TPU v7x, 32 devices: a whole 2x2x4 slice. The times are simulated.
32 devices in a mesh: horiz: 8 (over y, x, core), lev: 4 (over z).
Axes of the slice: x: 2, y: 2, z: 4, core: 2. Of those that a mesh axis runs over, the one named last changes fastest.
Arguments:
- source_state: bfloat16 [5, 68, 32768], P(None, 'lev', 'horiz'), may hold values from -6 to 6
- intersection: int32 [40], P('horiz'), may hold values from 0 to 7, as said below
- index_map: int32 [40, 512], P('horiz'), may hold values from 0 to 4095
- blocks: bfloat16 [40, 512, 2048], P('horiz'), may hold values from -0.125 to 0.125
- bracket: int32 [127, 16384], P(None, ('horiz', 'lev')), may hold values from 0 to 66
- fraction: float32 [127, 16384], P(None, ('horiz', 'lev')), may hold values from 0 to 1
Outputs:
- target_state: bfloat16 [5, 127, 16384], P(None, None, ('horiz', 'lev'))
Inputs may be any that keep to these rules, and one draw needn't show every extreme that they name: For every target group g, intersection[g * 5] to intersection[g * 5 + 4] are the groups g - 2 to g + 2 modulo 8, each once, in some order.
All inputs are finite; a program needn't handle non-finite values.
Results may differ from a plain program's by a relative error of at most 0.0049.
Values may be sent and summed in bfloat16 or wider, within the bound.
No kernel may reach another device: no remote copies, remote signals or barrier semaphores. Data moves between devices by JAX's collectives and lax.ppermute only.
A program may use at most 64 MiB of HBM per device.

v0:
```python
import jax
import jax.numpy as jnp
from jax import lax
from jax.sharding import PartitionSpec as P


def shifted(block, axis, distance):
    devices = range(lax.axis_size(axis))
    route = [((i - distance) % len(devices), i) for i in devices]
    return lax.ppermute(block, axis, route)


def select_cells(tile, wanted):
    cell_ids = jnp.arange(tile.shape[1], dtype=jnp.int32)[:, None]
    picker = (cell_ids == wanted[None, :]).astype(jnp.bfloat16)
    return jnp.dot(tile, picker, preferred_element_type=jnp.float32).astype(jnp.bfloat16)


def local(source_state, intersection, index_map, blocks, bracket, fraction):
    fields, level_slab, tile_cells = source_state.shape
    stacked = source_state.reshape(fields * level_slab, tile_cells)
    groups = lax.axis_size("horiz")
    block_count = intersection.shape[0]
    depth = (block_count - 1) // 2
    own_group = lax.axis_index("horiz")
    position = (intersection - own_group + depth) % groups
    collected = []
    for offset in range(-depth, depth + 1):
        wanted_group = (own_group + offset) % groups
        matched = intersection == wanted_group
        request = jnp.sum(jnp.where(matched[:, None], index_map, 0), axis=0)
        if offset == 0:
            collected.append(select_cells(stacked, request))
        else:
            incoming = shifted(request, "horiz", offset)
            outgoing = select_cells(stacked, incoming)
            collected.append(shifted(outgoing, "horiz", -offset))
    by_offset = jnp.stack(collected)
    pieces = [
        lax.dynamic_index_in_dim(by_offset, position[block_slot], 0, keepdims=False)
        for block_slot in range(block_count)
    ]
    chosen = jnp.concatenate(pieces, axis=1)
    weights_flat = blocks.reshape(-1, blocks.shape[2])
    horizontal = jnp.dot(chosen, weights_flat, preferred_element_type=jnp.float32).astype(
        jnp.bfloat16
    )
    horizontal = horizontal.reshape(fields, level_slab, blocks.shape[2])
    level_total = level_slab * lax.axis_size("lev")
    level_ids = jnp.arange(level_total, dtype=jnp.int32)[None, :, None]
    lower_hit = level_ids == bracket[:, None, :]
    upper_hit = level_ids == bracket[:, None, :] + 1
    upper_share = fraction[:, None, :]
    interp = jnp.where(lower_hit, 1.0 - upper_share, 0.0) + jnp.where(upper_hit, upper_share, 0.0)
    widened = lax.all_to_all(horizontal, "lev", split_axis=2, concat_axis=1, tiled=True).astype(
        jnp.float32
    )
    mixed = jnp.einsum("jlc,flc->fjc", interp, widened, precision=lax.Precision.HIGHEST)
    return mixed.astype(jnp.bfloat16)


def solution(mesh):
    in_specs = (
        P(None, "lev", "horiz"),
        P("horiz"),
        P("horiz", None),
        P("horiz", None, None),
        P(None, ("horiz", "lev")),
        P(None, ("horiz", "lev")),
    )
    out_specs = P(None, None, ("horiz", "lev"))
    return jax.shard_map(local, mesh=mesh, in_specs=in_specs, out_specs=out_specs, check_vma=False)
```

profile of v0, /device:TPU:0, one launch (start us, length us, event | category | flops | bytes accessed | tf_op | source)
XLA Modules:
  0.0 83.7 jit_solution(5691113030933345913)
XLA Ops:
  0.0 0.7 broadcast_compare_fusion.1
  0.7 0.8 select_reduce_fusion
  1.5 3.4 %collective-permute-start.2 = (s32[512]{0:T(512)S(1)}, s32[512]{0:T(512)S(1)}, u32[]{:S(2)}, u32[]{:S(2)}) collective-permute-start(s32[512]{0:T(512)S(1)} %get-tuple-element.7), channel_id=1, source_target_pairs={{4,0},{8,4},{12,8},{16,12},{20,16},{24,20},{28,24},{0,28},{5,1},{9... | collective-permute-start | bytes 6152 | tf_op jit(solution)/shard_map/ppermute | solution.py:10
  4.9 0.6 collective-permute-start
  5.5 0.2 collective-permute-start.4
  5.7 1.2 %collective-permute-start.6 = (s32[512]{0:T(512)S(1)}, s32[512]{0:T(512)S(1)}, u32[]{:S(2)}, u32[]{:S(2)}) collective-permute-start(s32[512]{0:T(512)S(1)} %get-tuple-element.5), channel_id=1, source_target_pairs={{24,0},{28,4},{0,8},{4,12},{8,16},{12,20},{16,24},{20,28},{25,1},{... | collective-permute-start | bytes 6152 | tf_op jit(solution)/shard_map/ppermute | solution.py:10
  6.9 0.7 and_select_fusion
  7.6 0.7 fusion.38
  14.7 1.4 %reshape.25 = bf16[85,4096]{1,0:T(8,128)(2,1)S(1)} reshape(bf16[5,17,4096]{2,1,0:T(8,128)(2,1)} %param.6) | data formatting | bytes 1392640 | tf_op jit(solution)/shard_map/reshape | solution.py:21
  19.4 1.5 %fusion.31 = bf16[85,512]{1,0:T(8,128)(2,1)S(1)} fusion(bf16[85,4096]{1,0:T(8,128)(2,1)S(1)} %reshape.25, s32[512]{0:T(512)S(1)} %collective-permute-done.2), kind=kOutput, calls=%fused_computation.35 | convolution fusion | flops 358656512 | bytes 785408 | tf_op jit(solution)/shard_map/dot_general | solution.py:16
  20.9 0.5 collective-permute-start.3
  21.3 1.5 %fusion.30 = bf16[85,512]{1,0:T(8,128)(2,1)S(1)} fusion(bf16[85,4096]{1,0:T(8,128)(2,1)S(1)} %reshape.25, s32[512]{0:T(512)S(1)} %collective-permute-done), kind=kOutput, calls=%fused_computation.34 | convolution fusion | flops 358656512 | bytes 785408 | tf_op jit(solution)/shard_map/dot_general | solution.py:16
  22.8 1.4 %collective-permute-start.1 = (bf16[85,512]{1,0:T(8,128)(2,1)S(1)}, bf16[85,512]{1,0:T(8,128)(2,1)S(1)}, u32[]{:S(2)}, u32[]{:S(2)}) collective-permute-start(bf16[85,512]{1,0:T(8,128)(2,1)S(1)} %fusion.30), channel_id=1, source_target_pairs={{24,0},{28,4},{0,8},{4,12},{8,16},{12,20},{16,24},{20,28},{25,1},{... | collective-permute-start | bytes 261128 | tf_op jit(solution)/shard_map/ppermute | solution.py:10
  24.2 1.5 %fusion.34 = bf16[85,512]{1,0:T(8,128)(2,1)S(1)} fusion(bf16[85,4096]{1,0:T(8,128)(2,1)S(1)} %reshape.25, s32[512]{0:T(512)S(1)} %collective-permute-done.4), kind=kOutput, calls=%fused_computation.38 | convolution fusion | flops 358656512 | bytes 785408 | tf_op jit(solution)/shard_map/dot_general | solution.py:16
  25.7 1.3 %collective-permute-start.5 = (bf16[85,512]{1,0:T(8,128)(2,1)S(1)}, bf16[85,512]{1,0:T(8,128)(2,1)S(1)}, u32[]{:S(2)}, u32[]{:S(2)}) collective-permute-start(bf16[85,512]{1,0:T(8,128)(2,1)S(1)} %fusion.34), channel_id=1, source_target_pairs={{4,0},{8,4},{12,8},{16,12},{20,16},{24,20},{28,24},{0,28},{5,1},{9... | collective-permute-start | bytes 261128 | tf_op jit(solution)/shard_map/ppermute | solution.py:10
  27.1 1.5 %fusion.35 = bf16[85,512]{1,0:T(8,128)(2,1)S(1)} fusion(bf16[85,4096]{1,0:T(8,128)(2,1)S(1)} %reshape.25, s32[512]{0:T(512)S(1)} %collective-permute-done.6), kind=kOutput, calls=%fused_computation.39 | convolution fusion | flops 358656512 | bytes 785408 | tf_op jit(solution)/shard_map/dot_general | solution.py:16
  28.6 1.3 %collective-permute-start.7 = (bf16[85,512]{1,0:T(8,128)(2,1)S(1)}, bf16[85,512]{1,0:T(8,128)(2,1)S(1)}, u32[]{:S(2)}, u32[]{:S(2)}) collective-permute-start(bf16[85,512]{1,0:T(8,128)(2,1)S(1)} %fusion.35), channel_id=1, source_target_pairs={{8,0},{12,4},{16,8},{20,12},{24,16},{28,20},{0,24},{4,28},{9,1},{1... | collective-permute-start | bytes 261128 | tf_op jit(solution)/shard_map/ppermute | solution.py:10
  29.9 1.5 %fusion.33 = bf16[5,85,512]{2,1,0:T(8,128)(2,1)S(1)} fusion(bf16[5,85,512]{2,1,0:T(8,128)(2,1)S(1)} %bitcast_dynamic-update-slice_fusion.7, bf16[85,4096]{1,0:T(8,128)(2,1)S(1)} %reshape.25, s32[512]{0:T(512)S(1)} %get-tuple-element.6), kind=kOutput, calls=%fused_computation.37 | convolution fusion | flops 358656512 | bytes 813056 | tf_op jit(solution)/shard_map/dot_general | solution.py:16
  31.5 1.7 %collective-permute-done.7 = bf16[85,512]{1,0:T(8,128)(2,1)S(1)} collective-permute-done((bf16[85,512]{1,0:T(8,128)(2,1)S(1)}, bf16[85,512]{1,0:T(8,128)(2,1)S(1)}, u32[]{:S(2)}, u32[]{:S(2)}) %collective-permute-start.7) | collective-permute-done | bytes 87072 | tf_op jit(solution)/shard_map/ppermute | solution.py:10
  33.3 1.9 %convolution_convert_fusion = bf16[85,2048]{1,0:T(8,128)(2,1)S(1)} fusion(bf16[85,2560]{1,0:T(8,128)(2,1)S(1)} %bitcast_dynamic-update-slice_fusion, bf16[2560,2048]{1,0:T(8,128)(2,1)S(1)} %bitcast.54), kind=kOutput, calls=%fused_computation.26 | convolution fusion | flops 891463680 | bytes 11269120 | tf_op jit(solution)/shard_map/dot_general | solution.py:45
  35.3 4.2 %copy.26 = bf16[5,17,2048]{1,0,2:T(8,128)(2,1)} copy(bf16[5,17,2048]{2,1,0:T(8,128)(2,1)S(1)} %reshape.27) | data formatting | bytes 696320 | tf_op jit(solution)/shard_map/reshape | solution.py:48
  39.5 5.9 %reshape.28 = bf16[4,2,21760]{2,1,0:T(2,128)(2,1)} reshape(bf16[2048,5,17]{2,1,0:T(8,128)(2,1)} %bitcast.55) | data formatting | bytes 696320
  45.4 4.9 %all-to-all-start = ((bf16[4,2,21760]{2,1,0:T(2,128)(2,1)}), bf16[4,2,21760]{2,1,0:T(2,128)(2,1)S(1)}, u32[]{:S(2)}, u32[]{:S(2)}) async-start(bf16[4,2,21760]{2,1,0:T(2,128)(2,1)} %reshape.28), calls=%async_computation | async-start | bytes 696320 | tf_op jit(solution)/shard_map/all_to_all | solution.py:55
  50.5 0.1 copy.30
  50.6 0.1 copy.29
  50.8 0.1 copy.31
  50.9 8.3 %all-to-all-done = bf16[4,2,21760]{2,1,0:T(2,128)(2,1)S(1)} async-done(((bf16[4,2,21760]{2,1,0:T(2,128)(2,1)}), bf16[4,2,21760]{2,1,0:T(2,128)(2,1)S(1)}, u32[]{:S(2)}, u32[]{:S(2)}) %all-to-all-start) | async-done | bytes 348192 | tf_op jit(solution)/shard_map/all_to_all | solution.py:55
  59.3 5.0 %reshape.29 = bf16[2048,5,17]{2,1,0:T(8,128)(2,1)} reshape(bf16[4,2,21760]{2,1,0:T(2,128)(2,1)S(1)} %all-to-all-done) | data formatting | bytes 696320
  64.2 4.2 %copy.35 = bf16[5,17,4,512]{3,2,1,0:T(4,128)(2,1)S(1)} copy(bf16[5,17,4,512]{1,0,3,2:T(8,128)(2,1)} %bitcast.56) | data formatting | bytes 696320 | tf_op jit(solution)/shard_map/all_to_all | solution.py:55
  68.7 0.8 copy.33
  69.4 12.9 %fusion.22 = bf16[5,127,512]{1,0,2:T(8,128)(2,1)S(1)} fusion(bf16[5,68,512]{1,0,2:T(8,128)(2,1)S(1)} %copy.33, f32[127,512]{0,1:T(8,128)S(1)} %copy.32, s32[127,512]{0,1:T(8,128)S(1)} %copy.31, f32[127,512]{0,1:T(8,128)S(1)} %copy.30, s32[127,512]{0,1:T(8,128)S(1)} %copy.29), kind=kOutput, calls=%fused_computation.28 | convolution fusion | flops 287731200 | bytes 2038784 | tf_op jit(solution)/shard_map/jlc,flc->fjc/dot_general | solution.py:58
  82.4 1.4 %copy.34 = bf16[5,127,512]{2,1,0:T(8,128)(2,1)} copy(bf16[5,127,512]{1,0,2:T(8,128)(2,1)S(1)} %fusion.22) | data formatting | bytes 1300480 | tf_op jit(solution)/shard_map/convert_element_type | solution.py:59
  (33 shorter events, 0.6 us)
Async XLA Ops:
  1.5 17.9 %collective-permute-start.2 = (s32[512]{0:T(512)S(1)}, s32[512]{0:T(512)S(1)}, u32[]{:S(2)}, u32[]{:S(2)}) collective-permute-start(s32[512]{0:T(512)S(1)} %get-tuple-element.7), channel_id=1, source_target_pairs={{4,0},{8,4},{12,8},{16,12},{20,16},{24,20},{28,24},{0,28},{5,1},{9... | collective-permute-start | bytes 6152 | tf_op jit(solution)/shard_map/ppermute | solution.py:10
  4.9 16.4 %collective-permute-start = (s32[512]{0:T(512)S(1)}, s32[512]{0:T(512)S(1)}, u32[]{:S(2)}, u32[]{:S(2)}) collective-permute-start(s32[512]{0:T(512)S(1)} %get-tuple-element.8), channel_id=1, source_target_pairs={{8,0},{12,4},{16,8},{20,12},{24,16},{28,20},{0,24},{4,28},{9,1},{1... | collective-permute-start | bytes 6152 | tf_op jit(solution)/shard_map/ppermute | solution.py:10
  5.5 18.7 %collective-permute-start.4 = (s32[512]{0:T(512)S(1)}, s32[512]{0:T(512)S(1)}, u32[]{:S(2)}, u32[]{:S(2)}) collective-permute-start(s32[512]{0:T(512)S(1)} %get-tuple-element.9), channel_id=1, source_target_pairs={{28,0},{0,4},{4,8},{8,12},{12,16},{16,20},{20,24},{24,28},{29,1},{... | collective-permute-start | bytes 6152 | tf_op jit(solution)/shard_map/ppermute | solution.py:10
  5.7 21.4 %collective-permute-start.6 = (s32[512]{0:T(512)S(1)}, s32[512]{0:T(512)S(1)}, u32[]{:S(2)}, u32[]{:S(2)}) collective-permute-start(s32[512]{0:T(512)S(1)} %get-tuple-element.5), channel_id=1, source_target_pairs={{24,0},{28,4},{0,8},{4,12},{8,16},{12,20},{16,24},{20,28},{25,1},{... | collective-permute-start | bytes 6152 | tf_op jit(solution)/shard_map/ppermute | solution.py:10
  19.3 13.9 %slice-start = ((s8[10485760]{0:T(1024)(128)(4,1)}), s8[4194304]{0:T(1024)(128)(4,1)S(1)}, s32[]{:S(2)}) async-start(s8[10485760]{0:T(1024)(128)(4,1)} %bitcast.52), calls=%async_computation.1 | async-start | bytes 8388608
  20.8 12.4 %slice-start.1 = ((s8[10485760]{0:T(1024)(128)(4,1)}), s8[4194304]{0:T(1024)(128)(4,1)S(1)}, s32[]{:S(2)}) async-start(s8[10485760]{0:T(1024)(128)(4,1)} %bitcast.52), calls=%async_computation.2 | async-start | bytes 8388608
  20.9 9.1 %collective-permute-start.3 = (bf16[85,512]{1,0:T(8,128)(2,1)S(1)}, bf16[85,512]{1,0:T(8,128)(2,1)S(1)}, u32[]{:S(2)}, u32[]{:S(2)}) collective-permute-start(bf16[85,512]{1,0:T(8,128)(2,1)S(1)} %fusion.31), channel_id=1, source_target_pairs={{28,0},{0,4},{4,8},{8,12},{12,16},{16,20},{20,24},{24,28},{29,1},{... | collective-permute-start | bytes 261128 | tf_op jit(solution)/shard_map/ppermute | solution.py:10
  22.8 7.1 %collective-permute-start.1 = (bf16[85,512]{1,0:T(8,128)(2,1)S(1)}, bf16[85,512]{1,0:T(8,128)(2,1)S(1)}, u32[]{:S(2)}, u32[]{:S(2)}) collective-permute-start(bf16[85,512]{1,0:T(8,128)(2,1)S(1)} %fusion.30), channel_id=1, source_target_pairs={{24,0},{28,4},{0,8},{4,12},{8,16},{12,20},{16,24},{20,28},{25,1},{... | collective-permute-start | bytes 261128 | tf_op jit(solution)/shard_map/ppermute | solution.py:10
  25.7 7.6 %slice-start.2 = ((s8[10485760]{0:T(1024)(128)(4,1)}), s8[2097152]{0:T(1024)(128)(4,1)S(1)}, s32[]{:S(2)}) async-start(s8[10485760]{0:T(1024)(128)(4,1)} %bitcast.52), calls=%async_computation.3 | async-start | bytes 4194304
  25.7 5.7 %collective-permute-start.5 = (bf16[85,512]{1,0:T(8,128)(2,1)S(1)}, bf16[85,512]{1,0:T(8,128)(2,1)S(1)}, u32[]{:S(2)}, u32[]{:S(2)}) collective-permute-start(bf16[85,512]{1,0:T(8,128)(2,1)S(1)} %fusion.34), channel_id=1, source_target_pairs={{4,0},{8,4},{12,8},{16,12},{20,16},{24,20},{28,24},{0,28},{5,1},{9... | collective-permute-start | bytes 261128 | tf_op jit(solution)/shard_map/ppermute | solution.py:10
  28.6 4.6 %collective-permute-start.7 = (bf16[85,512]{1,0:T(8,128)(2,1)S(1)}, bf16[85,512]{1,0:T(8,128)(2,1)S(1)}, u32[]{:S(2)}, u32[]{:S(2)}) collective-permute-start(bf16[85,512]{1,0:T(8,128)(2,1)S(1)} %fusion.35), channel_id=1, source_target_pairs={{8,0},{12,4},{16,8},{20,12},{24,16},{28,20},{0,24},{4,28},{9,1},{1... | collective-permute-start | bytes 261128 | tf_op jit(solution)/shard_map/ppermute | solution.py:10
  35.2 15.1 %copy-start = (f32[127,512]{1,0:T(8,128)S(1)}, f32[127,512]{1,0:T(8,128)}, u32[]{:S(2)}) copy-start(f32[127,512]{1,0:T(8,128)} %param.11) | copy-start | bytes 780292
  35.2 15.4 %copy-start.1 = (s32[127,512]{1,0:T(8,128)S(1)}, s32[127,512]{1,0:T(8,128)}, u32[]{:S(2)}) copy-start(s32[127,512]{1,0:T(8,128)} %param.10) | copy-start | bytes 780292
  45.4 13.8 %all-to-all-start = ((bf16[4,2,21760]{2,1,0:T(2,128)(2,1)}), bf16[4,2,21760]{2,1,0:T(2,128)(2,1)S(1)}, u32[]{:S(2)}, u32[]{:S(2)}) async-start(bf16[4,2,21760]{2,1,0:T(2,128)(2,1)} %reshape.28), calls=%async_computation | async-start | bytes 696320 | tf_op jit(solution)/shard_map/all_to_all | solution.py:55
where the time goes:
time: 84.6 us; the launch traced here: 83.7 us
  local copies, waits for them, and re-layouts  24.5 us (29%)
  matrix products  22.2 us (26%)
  starting transfers between devices  14.9 us (18%)
  waiting for transfers between devices  10 us (12%)
  between operations  9.9 us (12%)
  other arithmetic  2.19 us (3%)
    dot_general x1, matrix products, local(): jnp.einsum('jlc,flc->fjc', interp, widened, precision=lax.Precision.HIGHEST)  12.9 us
    unnamed x21, local copies, waits for them, and re-layouts  11.2 us
    ppermute x8, starting transfers between devices, shifted(): return lax.ppermute(block, axis, route)  10 us
    all_to_all x1, waiting for transfers between devices, local(): lax.all_to_all(horizontal, 'lev', split_axis=2, concat_axis=1, tiled=True)  8.33 us
    dot_general x5, matrix products, select_cells(): jnp.dot(tile, picker, preferred_element_type=jnp.float32)  7.4 us
    all_to_all x4, local copies, waits for them, and re-layouts, local(): lax.all_to_all(horizontal, 'lev', split_axis=2, concat_axis=1, tiled=True)  5.19 us
    all_to_all x1, starting transfers between devices, local(): lax.all_to_all(horizontal, 'lev', split_axis=2, concat_axis=1, tiled=True)  4.87 us
    reshape x2, local copies, waits for them, and re-layouts, local(): horizontal = horizontal.reshape(fields, level_slab, blocks.shape[2])  4.33 us
  transfers between devices with their start and end apart: 9, of which 2 were waited for; matrix products, arithmetic and copies ran while one was open for 13% of the time, Pallas kernels for 0%

commit v1 on v0

--- a/solution.py
+++ b/solution.py
@@ -1,7 +1,12 @@
 import jax
 import jax.numpy as jnp
 from jax import lax
+from jax.experimental import pallas as pl
+from jax.experimental.pallas import tpu as pltpu
 from jax.sharding import PartitionSpec as P
+
+SUB = 8
+LANES = 128
 
 
 def shifted(block, axis, distance):
@@ -14,6 +19,91 @@
     cell_ids = jnp.arange(tile.shape[1], dtype=jnp.int32)[:, None]
     picker = (cell_ids == wanted[None, :]).astype(jnp.bfloat16)
     return jnp.dot(tile, picker, preferred_element_type=jnp.float32).astype(jnp.bfloat16)
+
+
+def choose(values, bits):
+    for bit in bits:
+        pairs = [
+            jnp.where(bit, values[i + 1], values[i]) if i + 1 < len(values) else values[i]
+            for i in range(0, len(values), 2)
+        ]
+        values = pairs
+    return values[0]
+
+
+def interpolate_body(lower_ref, upper_ref, fraction_ref, *refs):
+    slab_refs, out_ref, held_ref = refs[:-2], refs[-2], refs[-1]
+    fields, levels_out, width = out_ref.shape
+    slab = slab_refs[0].shape[0] // fields
+    tiles = -(-len(slab_refs) * slab // SUB)
+    for place, slab_ref in enumerate(slab_refs):
+        rows = slab_ref[...].astype(jnp.float32)
+        for f in range(fields):
+            held_ref[f, place * slab : (place + 1) * slab, :] = rows[f * slab : (f + 1) * slab]
+    digits = max(1, (tiles - 1).bit_length())
+    step = 2 * SUB
+
+    def load(ref, first, size, cols):
+        value = ref[pl.ds(first, size), cols]
+        if size < SUB:
+            rest = jnp.zeros((SUB - size, LANES), value.dtype)
+            value = jnp.concatenate([value, rest], axis=0)
+        return value
+
+    def split(row):
+        tile = row >> 3
+        return row & (SUB - 1), [(tile & (1 << i)) != 0 for i in range(digits)]
+
+    def fetch(values, row):
+        index, bits = row
+        return choose(
+            [jnp.take_along_axis(v, index, axis=0, mode="promise_in_bounds") for v in values], bits
+        )
+
+    def band(first, count, col):
+        cols = pl.ds(col, LANES)
+        halves = []
+        for start in range(0, count, SUB):
+            size = min(SUB, count - start)
+            share = load(fraction_ref, first + start, size, cols)
+            below = split(load(lower_ref, first + start, size, cols))
+            above = split(load(upper_ref, first + start, size, cols))
+            halves.append((below, above, share, 1.0 - share))
+        for f in range(fields):
+            values = [held_ref[f, k * SUB : (k + 1) * SUB, cols] for k in range(tiles)]
+            results = [
+                rest * fetch(values, below) + share * fetch(values, above)
+                for below, above, share, rest in halves
+            ]
+            mixed = jnp.concatenate(results, axis=0)[:count]
+            out_ref[f, pl.ds(first, count), cols] = mixed.astype(jnp.bfloat16)
+
+    full = levels_out // step
+
+    @pl.loop(0, width // LANES)
+    def _(c):
+        col = pl.multiple_of(c * LANES, LANES)
+
+        @pl.loop(0, full)
+        def _(j):
+            band(pl.multiple_of(j * step, step), step, col)
+
+        if levels_out % step:
+            band(full * step, levels_out % step, col)
+
+
+def interpolate(lower, upper, fraction, slabs, fields):
+    rows, width = slabs[0].shape
+    held = -(-len(slabs) * rows // fields // SUB) * SUB
+    vmem = pl.BlockSpec(memory_space=pltpu.VMEM)
+    return pl.pallas_call(
+        interpolate_body,
+        out_shape=jax.ShapeDtypeStruct((fields, lower.shape[0], width), jnp.bfloat16),
+        in_specs=[vmem] * (3 + len(slabs)),
+        out_specs=vmem,
+        scratch_shapes=[pltpu.VMEM((fields, held, width), jnp.float32)],
+        name="interpolate",
+    )(lower, upper, fraction, *slabs)
 
 
 def local(source_state, intersection, index_map, blocks, bracket, fraction):
@@ -45,18 +135,19 @@
     horizontal = jnp.dot(chosen, weights_flat, preferred_element_type=jnp.float32).astype(
         jnp.bfloat16
     )
-    horizontal = horizontal.reshape(fields, level_slab, blocks.shape[2])
-    level_total = level_slab * lax.axis_size("lev")
-    level_ids = jnp.arange(level_total, dtype=jnp.int32)[None, :, None]
-    lower_hit = level_ids == bracket[:, None, :]
-    upper_hit = level_ids == bracket[:, None, :] + 1
-    upper_share = fraction[:, None, :]
-    interp = jnp.where(lower_hit, 1.0 - upper_share, 0.0) + jnp.where(upper_hit, upper_share, 0.0)
-    widened = lax.all_to_all(horizontal, "lev", split_axis=2, concat_axis=1, tiled=True).astype(
-        jnp.float32
-    )
-    mixed = jnp.einsum("jlc,flc->fjc", interp, widened, precision=lax.Precision.HIGHEST)
-    return mixed.astype(jnp.bfloat16)
+    shares = lax.axis_size("lev")
+    own_share = lax.axis_index("lev")
+    width = blocks.shape[2] // shares
+    slabs = []
+    for distance in range(shares):
+        target = (own_share + distance) % shares
+        part = lax.dynamic_slice_in_dim(horizontal, target * width, width, axis=1)
+        slabs.append(part if distance == 0 else shifted(part, "lev", distance))
+
+    def place(level):
+        return (own_share - level // level_slab) % shares * level_slab + level % level_slab
+
+    return interpolate(place(bracket), place(bracket + 1), fraction, slabs, fields)
 
 
 def solution(mesh):

time: 84.6 us -> 52.2 us (0.62)
  local copies, waits for them, and re-layouts: 24.5 us -> 3.53 us
  matrix products: 22.2 us -> 9.26 us
  Pallas kernels: 0 us -> 4.28 us
  waiting for transfers between devices: 10 us -> 6.94 us
  other arithmetic: 2.19 us -> 3.68 us
    dot_general x1 -> x0, matrix products: 12.9 us -> none  [local(): jnp.einsum('jlc,flc->fjc', interp, widened, precision=lax.Precision.HIGHEST)]
    unnamed x21, local copies, waits for them, and re-layouts: 11.2 us -> 0.74 us
    all_to_all x1 -> x0, waiting for transfers between devices: 8.33 us -> none  [local(): lax.all_to_all(horizontal, 'lev', split_axis=2, concat_axis=1, tiled=True)]
    ppermute x8 -> x11, waiting for transfers between devices: 1.71 us -> 6.94 us  [shifted(): return lax.ppermute(block, axis, route)]
    all_to_all x4 -> x0, local copies, waits for them, and re-layouts: 5.19 us -> none  [local(): lax.all_to_all(horizontal, 'lev', split_axis=2, concat_axis=1, tiled=True)]
    all_to_all x1 -> x0, starting transfers between devices: 4.87 us -> none  [local(): lax.all_to_all(horizontal, 'lev', split_axis=2, concat_axis=1, tiled=True)]
    ppermute x8 -> x11, starting transfers between devices: 10 us -> 14.7 us  [shifted(): return lax.ppermute(block, axis, route)]
    reshape x2 -> x0, local copies, waits for them, and re-layouts: 4.33 us -> none  [local(): horizontal = horizontal.reshape(fields, level_slab, blocks.shape[2])]
  transfers between devices with their start and end apart: 9 -> 11, of which waited for: 2 -> 3; matrix products, arithmetic and copies ran while one was open for 13% -> 23% of each run, Pallas kernels for 0% -> 0%
where the time goes in v1:
time: 52.2 us; the launch traced here: 51.9 us
  starting transfers between devices  14.7 us (28%)
  between operations  9.54 us (18%)
  matrix products  9.26 us (18%)
  waiting for transfers between devices  6.94 us (13%)
  Pallas kernels  4.28 us (8%)
  other arithmetic  3.68 us (7%)
  local copies, waits for them, and re-layouts  3.53 us (7%)
    ppermute x11, starting transfers between devices, shifted(): return lax.ppermute(block, axis, route)  14.7 us
    dot_general x5, matrix products, select_cells(): jnp.dot(tile, picker, preferred_element_type=jnp.float32)  7.4 us
    ppermute x11, waiting for transfers between devices, shifted(): return lax.ppermute(block, axis, route)  6.94 us
    pallas_call x1, Pallas kernels, interpolate(): pl.pallas_call(interpolate_body, out_shape=jax.ShapeDtypeStruct((fields,...  4.28 us
    dot_general x1, matrix products, local(): jnp.dot(chosen, weights_flat, preferred_element_type=jnp.float32)  1.86 us
    add x1, other arithmetic, place(): (own_share - level // level_slab) % shares * level_slab + level % level_slab  1.53 us
    reshape x1, local copies, waits for them, and re-layouts, local(): stacked = source_state.reshape(fields * level_slab, tile_cells)  1.45 us
  transfers between devices with their start and end apart: 11, of which 3 were waited for; matrix products, arithmetic and copies ran while one was open for 23% of the time, Pallas kernels for 0%

profile of v1, /device:TPU:0, one launch (start us, length us, event | category | flops | bytes accessed | tf_op | source)
XLA Modules:
  0.0 51.9 jit_solution(7785318849448975970)
XLA Ops:
  0.0 0.7 %broadcast_compare_fusion.1 = (pred[5]{0:T(512)(128)(4,1)S(1)}, pred[5]{0:T(512)(128)(4,1)S(1)}, pred[5]{0:T(512)(128)(4,1)S(1)}, pred[5]{0:T(512)(128)(4,1)S(1)}, pred[5]{0:T(512)(128)(4,1)S(1)}) fusion(s32[5]{0:T(128)} %param.7, s32[]{:T(128)S(6)} %select_n.127, s32[]{:T(128)S(6)} %select_n.125, s32[]{:T(128)S(6)} %select_n.123, s32[]{:T(128)S(6)} %select_n.121, ...), kind=kLoop, calls=%fused_computation.72 | loop fusion | flops 25 | bytes 65 | tf_op jit(solution)/shard_map/eq | solution.py:120
  0.7 0.8 %select_reduce_fusion = (s32[512]{0:T(512)S(1)}, s32[512]{0:T(512)S(1)}, s32[512]{0:T(512)S(1)}, s32[512]{0:T(512)S(1)}, s32[512]{0:T(512)S(1)}) fusion(s32[5,512]{1,0:T(8,128)} %param.8, pred[5]{0:T(512)(128)(4,1)S(1)} %get-tuple-element.25, pred[5]{0:T(512)(128)(4,1)S(1)} %get-tuple-element.22, pred[5]{0:T(512)(128)(4,1)S(1)} %get-tuple-element.23, ...), kind=kLoop, calls=%fused_computation.58 | loop fusion | flops 23040 | bytes 20505 | tf_op jit(solution)/shard_map/reduce_sum | solution.py:121
  1.5 3.4 %collective-permute-start.2 = (s32[512]{0:T(512)S(1)}, s32[512]{0:T(512)S(1)}, u32[]{:S(2)}, u32[]{:S(2)}) collective-permute-start(s32[512]{0:T(512)S(1)} %get-tuple-element.7), channel_id=1, source_target_pairs={{4,0},{8,4},{12,8},{16,12},{20,16},{24,20},{28,24},{0,28},{5,1},{9... | collective-permute-start | bytes 6152 | tf_op jit(solution)/shard_map/ppermute | solution.py:15
  4.9 0.6 %collective-permute-start = (s32[512]{0:T(512)S(1)}, s32[512]{0:T(512)S(1)}, u32[]{:S(2)}, u32[]{:S(2)}) collective-permute-start(s32[512]{0:T(512)S(1)} %get-tuple-element.8), channel_id=1, source_target_pairs={{8,0},{12,4},{16,8},{20,12},{24,16},{28,20},{0,24},{4,28},{9,1},{1... | collective-permute-start | bytes 6152 | tf_op jit(solution)/shard_map/ppermute | solution.py:15
  5.5 0.2 collective-permute-start.4
  5.7 1.2 %collective-permute-start.6 = (s32[512]{0:T(512)S(1)}, s32[512]{0:T(512)S(1)}, u32[]{:S(2)}, u32[]{:S(2)}) collective-permute-start(s32[512]{0:T(512)S(1)} %get-tuple-element.5), channel_id=1, source_target_pairs={{24,0},{28,4},{0,8},{4,12},{8,16},{12,20},{16,24},{20,28},{25,1},{... | collective-permute-start | bytes 6152 | tf_op jit(solution)/shard_map/ppermute | solution.py:15
  6.9 0.7 %and_select_fusion = s32[5]{0:T(128)S(1)} fusion(s32[5]{0:T(128)} %param.7, s32[]{:T(128)S(6)} %axis_index.25), kind=kLoop, calls=%fused_computation.69 | loop fusion | flops 65 | bytes 44 | tf_op jit(solution)/shard_map/jit(remainder)/select_n | solution.py:116
  7.6 0.6 %fusion.32 = (s32[1]{0:T(128)}, s32[1]{0:T(128)}, s32[1]{0:T(128)}, s32[1]{0:T(128)}, s32[1]{0:T(128)}) fusion(s32[5]{0:T(128)S(1)} %and_select_fusion), kind=kLoop, calls=%fused_computation.76 | loop fusion | bytes 40 | tf_op jit(solution)/shard_map/slice | solution.py:130
  14.5 1.4 %reshape.16 = bf16[85,4096]{1,0:T(8,128)(2,1)S(1)} reshape(bf16[5,17,4096]{2,1,0:T(8,128)(2,1)} %param.6) | data formatting | bytes 1392640 | tf_op jit(solution)/shard_map/reshape | solution.py:111
  19.1 0.0 slice-start
  19.1 1.5 %fusion.16 = bf16[85,512]{1,0:T(8,128)(2,1)S(1)} fusion(bf16[85,4096]{1,0:T(8,128)(2,1)S(1)} %reshape.16, s32[512]{0:T(512)S(1)} %collective-permute-done.2), kind=kOutput, calls=%fused_computation.22 | convolution fusion | flops 358656512 | bytes 785408 | tf_op jit(solution)/shard_map/dot_general | solution.py:21
  20.6 0.0 slice-start.1
  20.6 0.5 collective-permute-start.3
  21.0 1.5 %fusion.15 = bf16[85,512]{1,0:T(8,128)(2,1)S(1)} fusion(bf16[85,4096]{1,0:T(8,128)(2,1)S(1)} %reshape.16, s32[512]{0:T(512)S(1)} %collective-permute-done), kind=kOutput, calls=%fused_computation.21 | convolution fusion | flops 358656512 | bytes 785408 | tf_op jit(solution)/shard_map/dot_general | solution.py:21
  22.5 1.5 %collective-permute-start.1 = (bf16[85,512]{1,0:T(8,128)(2,1)S(1)}, bf16[85,512]{1,0:T(8,128)(2,1)S(1)}, u32[]{:S(2)}, u32[]{:S(2)}) collective-permute-start(bf16[85,512]{1,0:T(8,128)(2,1)S(1)} %fusion.15), channel_id=1, source_target_pairs={{24,0},{28,4},{0,8},{4,12},{8,16},{12,20},{16,24},{20,28},{25,1},{... | collective-permute-start | bytes 261128 | tf_op jit(solution)/shard_map/ppermute | solution.py:15
  24.0 1.5 %fusion.19 = bf16[85,512]{1,0:T(8,128)(2,1)S(1)} fusion(bf16[85,4096]{1,0:T(8,128)(2,1)S(1)} %reshape.16, s32[512]{0:T(512)S(1)} %collective-permute-done.4), kind=kOutput, calls=%fused_computation.25 | convolution fusion | flops 358656512 | bytes 785408 | tf_op jit(solution)/shard_map/dot_general | solution.py:21
  25.5 0.0 slice-start.2
  25.5 1.3 %collective-permute-start.5 = (bf16[85,512]{1,0:T(8,128)(2,1)S(1)}, bf16[85,512]{1,0:T(8,128)(2,1)S(1)}, u32[]{:S(2)}, u32[]{:S(2)}) collective-permute-start(bf16[85,512]{1,0:T(8,128)(2,1)S(1)} %fusion.19), channel_id=1, source_target_pairs={{4,0},{8,4},{12,8},{16,12},{20,16},{24,20},{28,24},{0,28},{5,1},{9... | collective-permute-start | bytes 261128 | tf_op jit(solution)/shard_map/ppermute | solution.py:15
  26.8 1.5 %fusion.20 = bf16[85,512]{1,0:T(8,128)(2,1)S(1)} fusion(bf16[85,4096]{1,0:T(8,128)(2,1)S(1)} %reshape.16, s32[512]{0:T(512)S(1)} %collective-permute-done.6), kind=kOutput, calls=%fused_computation.26 | convolution fusion | flops 358656512 | bytes 785408 | tf_op jit(solution)/shard_map/dot_general | solution.py:21
  28.3 1.3 %collective-permute-start.7 = (bf16[85,512]{1,0:T(8,128)(2,1)S(1)}, bf16[85,512]{1,0:T(8,128)(2,1)S(1)}, u32[]{:S(2)}, u32[]{:S(2)}) collective-permute-start(bf16[85,512]{1,0:T(8,128)(2,1)S(1)} %fusion.20), channel_id=1, source_target_pairs={{8,0},{12,4},{16,8},{20,12},{24,16},{28,20},{0,24},{4,28},{9,1},{1... | collective-permute-start | bytes 261128 | tf_op jit(solution)/shard_map/ppermute | solution.py:15
  29.7 1.5 %fusion.18 = bf16[5,85,512]{2,1,0:T(8,128)(2,1)S(1)} fusion(bf16[5,85,512]{2,1,0:T(8,128)(2,1)S(1)} %bitcast_dynamic-update-slice_fusion.7, bf16[85,4096]{1,0:T(8,128)(2,1)S(1)} %reshape.16, s32[512]{0:T(512)S(1)} %get-tuple-element.6), kind=kOutput, calls=%fused_computation.24 | convolution fusion | flops 358656512 | bytes 813056 | tf_op jit(solution)/shard_map/dot_general | solution.py:21
  31.2 1.7 %collective-permute-done.7 = bf16[85,512]{1,0:T(8,128)(2,1)S(1)} collective-permute-done((bf16[85,512]{1,0:T(8,128)(2,1)S(1)}, bf16[85,512]{1,0:T(8,128)(2,1)S(1)}, u32[]{:S(2)}, u32[]{:S(2)}) %collective-permute-start.7) | collective-permute-done | bytes 87072 | tf_op jit(solution)/shard_map/ppermute | solution.py:15
  33.0 0.0 copy-start
  33.1 1.9 %convolution_convert_fusion = bf16[85,2048]{1,0:T(8,128)(2,1)S(1)} fusion(bf16[85,2560]{1,0:T(8,128)(2,1)S(1)} %bitcast_dynamic-update-slice_fusion, bf16[2560,2048]{1,0:T(8,128)(2,1)S(1)} %bitcast.47), kind=kOutput, calls=%fused_computation.15 | convolution fusion | flops 891463680 | bytes 11269120 | tf_op jit(solution)/shard_map/dot_general | solution.py:135
  34.9 0.7 %constant_dynamic-slice_fusion = (bf16[85,512]{1,0:T(8,128)(2,1)S(1)}, bf16[85,512]{1,0:T(8,128)(2,1)S(1)}, bf16[85,512]{1,0:T(8,128)(2,1)S(1)}, bf16[85,512]{1,0:T(8,128)(2,1)}) fusion(bf16[85,2048]{1,0:T(8,128)(2,1)S(1)} %convolution_convert_fusion, s32[]{:T(128)S(6)} %select_n.144, s32[]{:T(128)S(6)} %select_n.142, s32[]{:T(128)S(6)} %select_n.140, ...), kind=kLoop, calls=%fused_computation.63 | loop fusion | bytes 696336 | tf_op jit(solution)/shard_map/dynamic_slice | solution.py:144
  35.6 3.6 %collective-permute-start.10 = (bf16[85,512]{1,0:T(8,128)(2,1)S(1)}, bf16[85,512]{1,0:T(8,128)(2,1)S(1)}, u32[]{:S(2)}, u32[]{:S(2)}) collective-permute-start(bf16[85,512]{1,0:T(8,128)(2,1)S(1)} %get-tuple-element.10), channel_id=1, source_target_pairs={{1,0},{2,1},{3,2},{0,3},{5,4},{6,5},{7,6},{4,7},{9,8},{10,9},{11,1... | collective-permute-start | bytes 261128 | tf_op jit(solution)/shard_map/ppermute | solution.py:15
  39.2 1.0 %collective-permute-start.9 = (bf16[85,512]{1,0:T(8,128)(2,1)S(1)}, bf16[85,512]{1,0:T(8,128)(2,1)S(1)}, u32[]{:S(2)}, u32[]{:S(2)}) collective-permute-start(bf16[85,512]{1,0:T(8,128)(2,1)S(1)} %get-tuple-element.11), channel_id=1, source_target_pairs={{2,0},{3,1},{0,2},{1,3},{6,4},{7,5},{4,6},{5,7},{10,8},{11,9},{8,1... | collective-permute-start | bytes 261128 | tf_op jit(solution)/shard_map/ppermute | solution.py:15
  40.2 1.5 %fusion.28 = (s32[127,512]{1,0:T(8,128)}, s32[127,512]{1,0:T(8,128)}) fusion(s32[127,512]{1,0:T(8,128)S(1)} %copy-done, s32[]{:T(128)S(6)} %axis_index.22), kind=kLoop, calls=%fused_computation.44 | loop fusion | flops 3446272 | bytes 780292 | tf_op jit(solution)/shard_map/add | solution.py:148
  41.7 3.8 %collective-permute-done.8.refs_1_ = bf16[85,512]{1,0:T(8,128)(2,1)S(1)} collective-permute-done((bf16[85,512]{1,0:T(8,128)(2,1)S(1)}, bf16[85,512]{1,0:T(8,128)(2,1)S(1)}, u32[]{:S(2)}, u32[]{:S(2)}) %collective-permute-start.8) | collective-permute-done | bytes 87072 | tf_op jit(solution)/shard_map/ppermute | solution.py:15
  45.5 1.4 %collective-permute-done.9.refs_2_ = bf16[85,512]{1,0:T(8,128)(2,1)S(1)} collective-permute-done((bf16[85,512]{1,0:T(8,128)(2,1)S(1)}, bf16[85,512]{1,0:T(8,128)(2,1)S(1)}, u32[]{:S(2)}, u32[]{:S(2)}) %collective-permute-start.9) | collective-permute-done | bytes 87072 | tf_op jit(solution)/shard_map/ppermute | solution.py:15
  47.0 0.6 %copy-done.3 = bf16[85,512]{1,0:T(8,128)(2,1)} copy-done((bf16[85,512]{1,0:T(8,128)(2,1)}, bf16[85,512]{1,0:T(8,128)(2,1)S(1)}, u32[]{:S(2)}) %copy-start.3) | copy-done | bytes 87064
  47.6 4.3 %interpolate.1 = bf16[5,127,512]{2,1,0:T(8,128)(2,1)} custom-call(s32[127,512]{1,0:T(8,128)} %get-tuple-element.15.lower_ref, s32[127,512]{1,0:T(8,128)} %get-tuple-element.14.upper_ref, f32[127,512]{1,0:T(8,128)} %fraction_ref.1, bf16[85,512]{1,0:T(8,128)(2,1)} %get-tuple-element.13.refs_0_, bf16[85,512]{1,0:T(8,128)(2,1)} %copy-done.2, ...), custom_call_target="tpu_custom_call" | custom-call | tf_op jit(solution)/shard_map/interpolate/pallas_call | solution.py:99
  (28 shorter events, 0.1 us)
Async XLA Ops:
  1.5 17.6 %collective-permute-start.2 = (s32[512]{0:T(512)S(1)}, s32[512]{0:T(512)S(1)}, u32[]{:S(2)}, u32[]{:S(2)}) collective-permute-start(s32[512]{0:T(512)S(1)} %get-tuple-element.7), channel_id=1, source_target_pairs={{4,0},{8,4},{12,8},{16,12},{20,16},{24,20},{28,24},{0,28},{5,1},{9... | collective-permute-start | bytes 6152 | tf_op jit(solution)/shard_map/ppermute | solution.py:15
  4.9 16.1 %collective-permute-start = (s32[512]{0:T(512)S(1)}, s32[512]{0:T(512)S(1)}, u32[]{:S(2)}, u32[]{:S(2)}) collective-permute-start(s32[512]{0:T(512)S(1)} %get-tuple-element.8), channel_id=1, source_target_pairs={{8,0},{12,4},{16,8},{20,12},{24,16},{28,20},{0,24},{4,28},{9,1},{1... | collective-permute-start | bytes 6152 | tf_op jit(solution)/shard_map/ppermute | solution.py:15
  5.5 18.4 %collective-permute-start.4 = (s32[512]{0:T(512)S(1)}, s32[512]{0:T(512)S(1)}, u32[]{:S(2)}, u32[]{:S(2)}) collective-permute-start(s32[512]{0:T(512)S(1)} %get-tuple-element.9), channel_id=1, source_target_pairs={{28,0},{0,4},{4,8},{8,12},{12,16},{16,20},{20,24},{24,28},{29,1},{... | collective-permute-start | bytes 6152 | tf_op jit(solution)/shard_map/ppermute | solution.py:15
  5.7 21.1 %collective-permute-start.6 = (s32[512]{0:T(512)S(1)}, s32[512]{0:T(512)S(1)}, u32[]{:S(2)}, u32[]{:S(2)}) collective-permute-start(s32[512]{0:T(512)S(1)} %get-tuple-element.5), channel_id=1, source_target_pairs={{24,0},{28,4},{0,8},{4,12},{8,16},{12,20},{16,24},{20,28},{25,1},{... | collective-permute-start | bytes 6152 | tf_op jit(solution)/shard_map/ppermute | solution.py:15
  19.1 13.9 %slice-start = ((s8[10485760]{0:T(1024)(128)(4,1)}), s8[4194304]{0:T(1024)(128)(4,1)S(1)}, s32[]{:S(2)}) async-start(s8[10485760]{0:T(1024)(128)(4,1)} %bitcast.45), calls=%async_computation | async-start | bytes 8388608
  20.6 12.4 %slice-start.1 = ((s8[10485760]{0:T(1024)(128)(4,1)}), s8[4194304]{0:T(1024)(128)(4,1)S(1)}, s32[]{:S(2)}) async-start(s8[10485760]{0:T(1024)(128)(4,1)} %bitcast.45), calls=%async_computation.1 | async-start | bytes 8388608
  20.6 9.1 %collective-permute-start.3 = (bf16[85,512]{1,0:T(8,128)(2,1)S(1)}, bf16[85,512]{1,0:T(8,128)(2,1)S(1)}, u32[]{:S(2)}, u32[]{:S(2)}) collective-permute-start(bf16[85,512]{1,0:T(8,128)(2,1)S(1)} %fusion.16), channel_id=1, source_target_pairs={{28,0},{0,4},{4,8},{8,12},{12,16},{16,20},{20,24},{24,28},{29,1},{... | collective-permute-start | bytes 261128 | tf_op jit(solution)/shard_map/ppermute | solution.py:15
  22.5 7.1 %collective-permute-start.1 = (bf16[85,512]{1,0:T(8,128)(2,1)S(1)}, bf16[85,512]{1,0:T(8,128)(2,1)S(1)}, u32[]{:S(2)}, u32[]{:S(2)}) collective-permute-start(bf16[85,512]{1,0:T(8,128)(2,1)S(1)} %fusion.15), channel_id=1, source_target_pairs={{24,0},{28,4},{0,8},{4,12},{8,16},{12,20},{16,24},{20,28},{25,1},{... | collective-permute-start | bytes 261128 | tf_op jit(solution)/shard_map/ppermute | solution.py:15
  25.5 7.6 %slice-start.2 = ((s8[10485760]{0:T(1024)(128)(4,1)}), s8[2097152]{0:T(1024)(128)(4,1)S(1)}, s32[]{:S(2)}) async-start(s8[10485760]{0:T(1024)(128)(4,1)} %bitcast.45), calls=%async_computation.2 | async-start | bytes 4194304
  25.5 5.7 %collective-permute-start.5 = (bf16[85,512]{1,0:T(8,128)(2,1)S(1)}, bf16[85,512]{1,0:T(8,128)(2,1)S(1)}, u32[]{:S(2)}, u32[]{:S(2)}) collective-permute-start(bf16[85,512]{1,0:T(8,128)(2,1)S(1)} %fusion.19), channel_id=1, source_target_pairs={{4,0},{8,4},{12,8},{16,12},{20,16},{24,20},{28,24},{0,28},{5,1},{9... | collective-permute-start | bytes 261128 | tf_op jit(solution)/shard_map/ppermute | solution.py:15
  28.3 4.6 %collective-permute-start.7 = (bf16[85,512]{1,0:T(8,128)(2,1)S(1)}, bf16[85,512]{1,0:T(8,128)(2,1)S(1)}, u32[]{:S(2)}, u32[]{:S(2)}) collective-permute-start(bf16[85,512]{1,0:T(8,128)(2,1)S(1)} %fusion.20), channel_id=1, source_target_pairs={{8,0},{12,4},{16,8},{20,12},{24,16},{28,20},{0,24},{4,28},{9,1},{1... | collective-permute-start | bytes 261128 | tf_op jit(solution)/shard_map/ppermute | solution.py:15
  33.0 7.2 %copy-start = (s32[127,512]{1,0:T(8,128)S(1)}, s32[127,512]{1,0:T(8,128)}, u32[]{:S(2)}) copy-start(s32[127,512]{1,0:T(8,128)} %param.10) | copy-start | bytes 780292
  35.6 6.2 %collective-permute-start.10 = (bf16[85,512]{1,0:T(8,128)(2,1)S(1)}, bf16[85,512]{1,0:T(8,128)(2,1)S(1)}, u32[]{:S(2)}, u32[]{:S(2)}) collective-permute-start(bf16[85,512]{1,0:T(8,128)(2,1)S(1)} %get-tuple-element.10), channel_id=1, source_target_pairs={{1,0},{2,1},{3,2},{0,3},{5,4},{6,5},{7,6},{4,7},{9,8},{10,9},{11,1... | collective-permute-start | bytes 261128 | tf_op jit(solution)/shard_map/ppermute | solution.py:15
  39.2 6.3 %collective-permute-start.8 = (bf16[85,512]{1,0:T(8,128)(2,1)S(1)}, bf16[85,512]{1,0:T(8,128)(2,1)S(1)}, u32[]{:S(2)}, u32[]{:S(2)}) collective-permute-start(bf16[85,512]{1,0:T(8,128)(2,1)S(1)} %get-tuple-element.12), channel_id=1, source_target_pairs={{3,0},{0,1},{1,2},{2,3},{7,4},{4,5},{5,6},{6,7},{11,8},{8,9},{9,10... | collective-permute-start | bytes 261128 | tf_op jit(solution)/shard_map/ppermute | solution.py:15
  39.2 7.8 %collective-permute-start.9 = (bf16[85,512]{1,0:T(8,128)(2,1)S(1)}, bf16[85,512]{1,0:T(8,128)(2,1)S(1)}, u32[]{:S(2)}, u32[]{:S(2)}) collective-permute-start(bf16[85,512]{1,0:T(8,128)(2,1)S(1)} %get-tuple-element.11), channel_id=1, source_target_pairs={{2,0},{3,1},{0,2},{1,3},{6,4},{7,5},{4,6},{5,7},{10,8},{11,9},{8,1... | collective-permute-start | bytes 261128 | tf_op jit(solution)/shard_map/ppermute | solution.py:15
  41.7 5.2 %copy-start.1 = (bf16[85,512]{1,0:T(8,128)(2,1)}, bf16[85,512]{1,0:T(8,128)(2,1)S(1)}, u32[]{:S(2)}) copy-start(bf16[85,512]{1,0:T(8,128)(2,1)S(1)} %collective-permute-done.10.refs_3_) | copy-start | bytes 261124
  45.5 1.5 %copy-start.2 = (bf16[85,512]{1,0:T(8,128)(2,1)}, bf16[85,512]{1,0:T(8,128)(2,1)S(1)}, u32[]{:S(2)}) copy-start(bf16[85,512]{1,0:T(8,128)(2,1)S(1)} %collective-permute-done.8.refs_1_) | copy-start | bytes 261124
  47.0 0.6 %copy-start.3 = (bf16[85,512]{1,0:T(8,128)(2,1)}, bf16[85,512]{1,0:T(8,128)(2,1)S(1)}, u32[]{:S(2)}) copy-start(bf16[85,512]{1,0:T(8,128)(2,1)S(1)} %collective-permute-done.9.refs_2_) | copy-start | bytes 261124

commit v2 on v1

--- a/solution.py
+++ b/solution.py
@@ -32,12 +32,12 @@
 
 
 def interpolate_body(lower_ref, upper_ref, fraction_ref, *refs):
-    slab_refs, out_ref, held_ref = refs[:-2], refs[-2], refs[-1]
+    sources, out_ref, held_ref = refs[:-2], refs[-2], refs[-1]
     fields, levels_out, width = out_ref.shape
-    slab = slab_refs[0].shape[0] // fields
-    tiles = -(-len(slab_refs) * slab // SUB)
-    for place, slab_ref in enumerate(slab_refs):
-        rows = slab_ref[...].astype(jnp.float32)
+    slab = sources[0].shape[0] // fields
+    tiles = -(-len(sources) * slab // SUB)
+    for place, source in enumerate(sources):
+        rows = source[...].astype(jnp.float32)
         for f in range(fields):
             held_ref[f, place * slab : (place + 1) * slab, :] = rows[f * slab : (f + 1) * slab]
     digits = max(1, (tiles - 1).bit_length())
@@ -125,12 +125,10 @@
             incoming = shifted(request, "horiz", offset)
             outgoing = select_cells(stacked, incoming)
             collected.append(shifted(outgoing, "horiz", -offset))
-    by_offset = jnp.stack(collected)
-    pieces = [
-        lax.dynamic_index_in_dim(by_offset, position[block_slot], 0, keepdims=False)
-        for block_slot in range(block_count)
-    ]
-    chosen = jnp.concatenate(pieces, axis=1)
+    reach = jnp.repeat(position, index_map.shape[1])[None, :]
+    chosen = jnp.zeros((stacked.shape[0], reach.shape[1]), jnp.bfloat16)
+    for place, piece in enumerate(collected):
+        chosen = jnp.where(reach == place, jnp.concatenate([piece] * block_count, axis=1), chosen)
     weights_flat = blocks.reshape(-1, blocks.shape[2])
     horizontal = jnp.dot(chosen, weights_flat, preferred_element_type=jnp.float32).astype(
         jnp.bfloat16

time: 52.2 us -> 43.8 us (0.84)
  between operations: 9.54 us -> 0.36 us
  waiting for transfers between devices: 6.94 us -> 8.54 us
  other arithmetic: 3.68 us -> 3.05 us
    ppermute x11, waiting for transfers between devices: 6.94 us -> 8.54 us  [shifted(): return lax.ppermute(block, axis, route)]
    select_n x1 -> x0, other arithmetic: 0.67 us -> none  [local(): position = (intersection - own_group + depth) % groups]
    slice x1 -> x0, local copies, waits for them, and re-layouts: 0.65 us -> none  [local(): position[block_slot]]
  transfers between devices with their start and end apart: 11 -> 11, of which waited for: 3 -> 3; matrix products, arithmetic and copies ran while one was open for 23% -> 25% of each run, Pallas kernels for 0% -> 0%
where the time goes in v2:
time: 43.8 us; the launch traced here: 43.6 us
  starting transfers between devices  14.7 us (34%)
  matrix products  9.28 us (21%)
  waiting for transfers between devices  8.54 us (19%)
  Pallas kernels  4.28 us (10%)
  local copies, waits for them, and re-layouts  3.44 us (8%)
  other arithmetic  3.05 us (7%)
    ppermute x11, starting transfers between devices, shifted(): return lax.ppermute(block, axis, route)  14.7 us
    ppermute x11, waiting for transfers between devices, shifted(): return lax.ppermute(block, axis, route)  8.54 us
    dot_general x5, matrix products, select_cells(): jnp.dot(tile, picker, preferred_element_type=jnp.float32)  7.4 us
    pallas_call x1, Pallas kernels, interpolate(): pl.pallas_call(interpolate_body, out_shape=jax.ShapeDtypeStruct((fields,...  4.28 us
    dot_general x1, matrix products, local(): jnp.dot(chosen, weights_flat, preferred_element_type=jnp.float32)  1.88 us
    add x1, other arithmetic, place(): (own_share - level // level_slab) % shares * level_slab + level % level_slab  1.54 us
    reshape x1, local copies, waits for them, and re-layouts, local(): stacked = source_state.reshape(fields * level_slab, tile_cells)  1.45 us
  transfers between devices with their start and end apart: 11, of which 3 were waited for; matrix products, arithmetic and copies ran while one was open for 25% of the time, Pallas kernels for 0%

profile of v2, /device:TPU:0, one launch (start us, length us, event | category | flops | bytes accessed | tf_op | source)
XLA Modules:
  0.0 43.6 jit_solution(12602482490571264525)
XLA Ops:
  0.0 0.7 %broadcast_compare_fusion.7 = (pred[5]{0:T(512)(128)(4,1)S(1)}, s32[5]{0:T(128)S(1)}, pred[5]{0:T(512)(128)(4,1)S(1)}, pred[5]{0:T(512)(128)(4,1)S(1)}, pred[5]{...) fusion(s32[5]{0:T(128)} %param.7, s32[]{:T(128)S(6)} %axis_index.25, s32[]{:T(128)S(6)} %select_n.126, ...), kind=kLoop, calls=%fused_computation.104 | loop fusion | flops 95 | bytes 94 | tf_op jit(solution)/shard_map/eq | solution.py:131
  0.7 0.8 %select_reduce_fusion = (s32[512]{0:T(512)S(1)}, s32[512]{0:T(512)S(1)}, s32[512]{0:T(512)S(1)}, s32[512]{0:T(512)S(1)}, s32[512]{0:T(512)S(1)}) fusion(s32[5,512]{1,0:T(8,128)} %param.8, pred[5]{0:T(512)(128)(4,1)S(1)} %get-tuple-element.25, pred[5]{0:T(512)(128)(4,1)S(1)} %get-tuple-element.22, pred[5]{0:T(512)(128)(4,1)S(1)} %get-tuple-element.23, ...), kind=kLoop, calls=%fused_computation.84 | loop fusion | flops 23040 | bytes 20505 | tf_op jit(solution)/shard_map/reduce_sum | solution.py:121
  1.5 4.0 %collective-permute-start.6 = (s32[512]{0:T(512)S(1)}, s32[512]{0:T(512)S(1)}, u32[]{:S(2)}, u32[]{:S(2)}) collective-permute-start(s32[512]{0:T(512)S(1)} %get-tuple-element.5), channel_id=1, source_target_pairs={{8,0},{12,4},{16,8},{20,12},{24,16},{28,20},{0,24},{4,28},{9,1},{1... | collective-permute-start | bytes 6152 | tf_op jit(solution)/shard_map/ppermute | solution.py:15
  5.5 0.5 %collective-permute-start.2 = (s32[512]{0:T(512)S(1)}, s32[512]{0:T(512)S(1)}, u32[]{:S(2)}, u32[]{:S(2)}) collective-permute-start(s32[512]{0:T(512)S(1)} %get-tuple-element.7), channel_id=1, source_target_pairs={{28,0},{0,4},{4,8},{8,12},{12,16},{16,20},{20,24},{24,28},{29,1},{... | collective-permute-start | bytes 6152 | tf_op jit(solution)/shard_map/ppermute | solution.py:15
  6.0 0.7 %collective-permute-start = (s32[512]{0:T(512)S(1)}, s32[512]{0:T(512)S(1)}, u32[]{:S(2)}, u32[]{:S(2)}) collective-permute-start(s32[512]{0:T(512)S(1)} %get-tuple-element.8), channel_id=1, source_target_pairs={{24,0},{28,4},{0,8},{4,12},{8,16},{12,20},{16,24},{20,28},{25,1},{... | collective-permute-start | bytes 6152 | tf_op jit(solution)/shard_map/ppermute | solution.py:15
  6.7 1.4 %reshape.61 = bf16[85,4096]{1,0:T(8,128)(2,1)S(1)} reshape(bf16[5,17,4096]{2,1,0:T(8,128)(2,1)} %param.6) | data formatting | bytes 1392640 | tf_op jit(solution)/shard_map/reshape | solution.py:111
  8.1 0.0 slice-start
  8.1 1.5 %constant_dynamic-update-slice_fusion.14 = (bf16[85,2560]{1,0:T(8,128)(2,1)S(1)}, bf16[85,512]{1,0:T(8,128)(2,1)S(1)}) fusion(bf16[85,4096]{1,0:T(8,128)(2,1)S(1)} %reshape.61, s32[512]{0:T(512)S(1)} %get-tuple-element.6), kind=kOutput, calls=%fused_computation.73 | convolution fusion | flops 358656512 | bytes 878592 | tf_op jit(solution)/shard_map/dot_general | solution.py:21
  9.7 0.1 broadcast_in_dim.97
  9.8 0.1 broadcast_in_dim.100
  9.9 0.1 broadcast_in_dim.103
  10.0 0.1 broadcast_in_dim.106
  10.1 0.1 broadcast_in_dim.93
  10.2 0.0 slice-start.1
  10.2 1.5 %fusion.19 = bf16[85,512]{1,0:T(8,128)(2,1)S(1)} fusion(bf16[85,4096]{1,0:T(8,128)(2,1)S(1)} %reshape.61, s32[512]{0:T(512)S(1)} %collective-permute-done.6), kind=kOutput, calls=%fused_computation.25 | convolution fusion | flops 358656512 | bytes 785408 | tf_op jit(solution)/shard_map/dot_general | solution.py:21
  11.7 1.3 %collective-permute-start.7 = (bf16[85,512]{1,0:T(8,128)(2,1)S(1)}, bf16[85,512]{1,0:T(8,128)(2,1)S(1)}, u32[]{:S(2)}, u32[]{:S(2)}) collective-permute-start(bf16[85,512]{1,0:T(8,128)(2,1)S(1)} %fusion.19), channel_id=1, source_target_pairs={{24,0},{28,4},{0,8},{4,12},{8,16},{12,20},{16,24},{20,28},{25,1},{... | collective-permute-start | bytes 261128 | tf_op jit(solution)/shard_map/ppermute | solution.py:15
  13.1 1.5 %fusion.18 = bf16[85,512]{1,0:T(8,128)(2,1)S(1)} fusion(bf16[85,4096]{1,0:T(8,128)(2,1)S(1)} %reshape.61, s32[512]{0:T(512)S(1)} %collective-permute-done.4), kind=kOutput, calls=%fused_computation.24 | convolution fusion | flops 358656512 | bytes 785408 | tf_op jit(solution)/shard_map/dot_general | solution.py:21
  14.6 0.3 collective-permute-start.5
  14.8 1.5 %fusion.16 = bf16[85,512]{1,0:T(8,128)(2,1)S(1)} fusion(bf16[85,4096]{1,0:T(8,128)(2,1)S(1)} %reshape.61, s32[512]{0:T(512)S(1)} %collective-permute-done.2), kind=kOutput, calls=%fused_computation.22 | convolution fusion | flops 358656512 | bytes 785408 | tf_op jit(solution)/shard_map/dot_general | solution.py:21
  16.3 2.5 %collective-permute-start.3 = (bf16[85,512]{1,0:T(8,128)(2,1)S(1)}, bf16[85,512]{1,0:T(8,128)(2,1)S(1)}, u32[]{:S(2)}, u32[]{:S(2)}) collective-permute-start(bf16[85,512]{1,0:T(8,128)(2,1)S(1)} %fusion.16), channel_id=1, source_target_pairs={{4,0},{8,4},{12,8},{16,12},{20,16},{24,20},{28,24},{0,28},{5,1},{9... | collective-permute-start | bytes 261128 | tf_op jit(solution)/shard_map/ppermute | solution.py:15
  18.8 1.5 %fusion.15 = bf16[85,512]{1,0:T(8,128)(2,1)S(1)} fusion(bf16[85,4096]{1,0:T(8,128)(2,1)S(1)} %reshape.61, s32[512]{0:T(512)S(1)} %collective-permute-done), kind=kOutput, calls=%fused_computation.21 | convolution fusion | flops 358656512 | bytes 785408 | tf_op jit(solution)/shard_map/dot_general | solution.py:21
  20.3 0.8 %collective-permute-start.1 = (bf16[85,512]{1,0:T(8,128)(2,1)S(1)}, bf16[85,512]{1,0:T(8,128)(2,1)S(1)}, u32[]{:S(2)}, u32[]{:S(2)}) collective-permute-start(bf16[85,512]{1,0:T(8,128)(2,1)S(1)} %fusion.15), channel_id=1, source_target_pairs={{8,0},{12,4},{16,8},{20,12},{24,16},{28,20},{0,24},{4,28},{9,1},{1... | collective-permute-start | bytes 261128 | tf_op jit(solution)/shard_map/ppermute | solution.py:15
  21.3 3.5 %collective-permute-done.1 = bf16[85,512]{1,0:T(8,128)(2,1)S(1)} collective-permute-done((bf16[85,512]{1,0:T(8,128)(2,1)S(1)}, bf16[85,512]{1,0:T(8,128)(2,1)S(1)}, u32[]{:S(2)}, u32[]{:S(2)}) %collective-permute-start.1) | collective-permute-done | bytes 87072 | tf_op jit(solution)/shard_map/ppermute | solution.py:15
  25.0 1.9 %convolution_convert_fusion = bf16[85,2048]{1,0:T(8,128)(2,1)S(1)} fusion(bf16[2560,2048]{1,0:T(8,128)(2,1)S(1)} %bitcast.19, bf16[85,2560]{1,0:T(8,128)(2,1)S(1)} %constant_dynamic-update-slice_fusion, bf16[85,2560]{1,0:T(8,128)(2,1)S(1)} %constant_dynamic-update-slice_fusion.5, bf16[85,2560]{1,0:T(8,128)(2,1)S(1)} %constant_dynamic-update-slice_fusion.10, ...), kind=kOutput, calls=%fused_computation.15 | convolution fusion | flops 892551680 | bytes 13022720 | tf_op jit(solution)/shard_map/dot_general | solution.py:133
  26.9 0.7 %constant_dynamic-slice_fusion = (bf16[85,512]{1,0:T(8,128)(2,1)S(1)}, bf16[85,512]{1,0:T(8,128)(2,1)S(1)}, bf16[85,512]{1,0:T(8,128)(2,1)S(1)}, bf16[85,512]{1,0:T(8,128)(2,1)}) fusion(bf16[85,2048]{1,0:T(8,128)(2,1)S(1)} %convolution_convert_fusion, s32[]{:T(128)S(6)} %select_n.144, s32[]{:T(128)S(6)} %select_n.142, s32[]{:T(128)S(6)} %select_n.140, ...), kind=kLoop, calls=%fused_computation.92 | loop fusion | bytes 696336 | tf_op jit(solution)/shard_map/dynamic_slice | solution.py:142
  27.5 3.6 %collective-permute-start.10 = (bf16[85,512]{1,0:T(8,128)(2,1)S(1)}, bf16[85,512]{1,0:T(8,128)(2,1)S(1)}, u32[]{:S(2)}, u32[]{:S(2)}) collective-permute-start(bf16[85,512]{1,0:T(8,128)(2,1)S(1)} %get-tuple-element.12), channel_id=1, source_target_pairs={{1,0},{2,1},{3,2},{0,3},{5,4},{6,5},{7,6},{4,7},{9,8},{10,9},{11,1... | collective-permute-start | bytes 261128 | tf_op jit(solution)/shard_map/ppermute | solution.py:15
  31.1 1.0 %collective-permute-start.9 = (bf16[85,512]{1,0:T(8,128)(2,1)S(1)}, bf16[85,512]{1,0:T(8,128)(2,1)S(1)}, u32[]{:S(2)}, u32[]{:S(2)}) collective-permute-start(bf16[85,512]{1,0:T(8,128)(2,1)S(1)} %get-tuple-element.13), channel_id=1, source_target_pairs={{2,0},{3,1},{0,2},{1,3},{6,4},{7,5},{4,6},{5,7},{10,8},{11,9},{8,1... | collective-permute-start | bytes 261128 | tf_op jit(solution)/shard_map/ppermute | solution.py:15
  32.1 1.5 %fusion.37 = (s32[127,512]{1,0:T(8,128)}, s32[127,512]{1,0:T(8,128)}) fusion(s32[127,512]{1,0:T(8,128)S(1)} %copy-done, s32[]{:T(128)S(6)} %axis_index.22), kind=kLoop, calls=%fused_computation.53 | loop fusion | flops 3446272 | bytes 780292 | tf_op jit(solution)/shard_map/add | solution.py:146
  33.7 3.9 %collective-permute-done.8.refs_1_ = bf16[85,512]{1,0:T(8,128)(2,1)S(1)} collective-permute-done((bf16[85,512]{1,0:T(8,128)(2,1)S(1)}, bf16[85,512]{1,0:T(8,128)(2,1)S(1)}, u32[]{:S(2)}, u32[]{:S(2)}) %collective-permute-start.8) | collective-permute-done | bytes 87072 | tf_op jit(solution)/shard_map/ppermute | solution.py:15
  37.6 1.1 %collective-permute-done.9.refs_2_ = bf16[85,512]{1,0:T(8,128)(2,1)S(1)} collective-permute-done((bf16[85,512]{1,0:T(8,128)(2,1)S(1)}, bf16[85,512]{1,0:T(8,128)(2,1)S(1)}, u32[]{:S(2)}, u32[]{:S(2)}) %collective-permute-start.9) | collective-permute-done | bytes 87072 | tf_op jit(solution)/shard_map/ppermute | solution.py:15
  38.7 0.6 %copy-done.3 = bf16[85,512]{1,0:T(8,128)(2,1)} copy-done((bf16[85,512]{1,0:T(8,128)(2,1)}, bf16[85,512]{1,0:T(8,128)(2,1)S(1)}, u32[]{:S(2)}) %copy-start.3) | copy-done | bytes 87064
  39.3 4.3 %interpolate.1 = bf16[5,127,512]{2,1,0:T(8,128)(2,1)} custom-call(s32[127,512]{1,0:T(8,128)} %get-tuple-element.17.lower_ref, s32[127,512]{1,0:T(8,128)} %get-tuple-element.16.upper_ref, f32[127,512]{1,0:T(8,128)} %fraction_ref.1, bf16[85,512]{1,0:T(8,128)(2,1)} %get-tuple-element.15.refs_0_, bf16[85,512]{1,0:T(8,128)(2,1)} %copy-done.2, ...), custom_call_target="tpu_custom_call" | custom-call | tf_op jit(solution)/shard_map/interpolate/pallas_call | solution.py:99
  (52 shorter events, 0.4 us)
Async XLA Ops:
  1.5 8.7 %collective-permute-start.6 = (s32[512]{0:T(512)S(1)}, s32[512]{0:T(512)S(1)}, u32[]{:S(2)}, u32[]{:S(2)}) collective-permute-start(s32[512]{0:T(512)S(1)} %get-tuple-element.5), channel_id=1, source_target_pairs={{8,0},{12,4},{16,8},{20,12},{24,16},{28,20},{0,24},{4,28},{9,1},{1... | collective-permute-start | bytes 6152 | tf_op jit(solution)/shard_map/ppermute | solution.py:15
  5.5 7.6 %collective-permute-start.4 = (s32[512]{0:T(512)S(1)}, s32[512]{0:T(512)S(1)}, u32[]{:S(2)}, u32[]{:S(2)}) collective-permute-start(s32[512]{0:T(512)S(1)} %get-tuple-element.9), channel_id=1, source_target_pairs={{4,0},{8,4},{12,8},{16,12},{20,16},{24,20},{28,24},{0,28},{5,1},{9... | collective-permute-start | bytes 6152 | tf_op jit(solution)/shard_map/ppermute | solution.py:15
  5.5 9.4 %collective-permute-start.2 = (s32[512]{0:T(512)S(1)}, s32[512]{0:T(512)S(1)}, u32[]{:S(2)}, u32[]{:S(2)}) collective-permute-start(s32[512]{0:T(512)S(1)} %get-tuple-element.7), channel_id=1, source_target_pairs={{28,0},{0,4},{4,8},{8,12},{12,16},{16,20},{20,24},{24,28},{29,1},{... | collective-permute-start | bytes 6152 | tf_op jit(solution)/shard_map/ppermute | solution.py:15
  6.0 12.8 %collective-permute-start = (s32[512]{0:T(512)S(1)}, s32[512]{0:T(512)S(1)}, u32[]{:S(2)}, u32[]{:S(2)}) collective-permute-start(s32[512]{0:T(512)S(1)} %get-tuple-element.8), channel_id=1, source_target_pairs={{24,0},{28,4},{0,8},{4,12},{8,16},{12,20},{16,24},{20,28},{25,1},{... | collective-permute-start | bytes 6152 | tf_op jit(solution)/shard_map/ppermute | solution.py:15
  8.1 16.8 %slice-start = ((s8[10485760]{0:T(1024)(128)(4,1)}), s8[2097152]{0:T(1024)(128)(4,1)S(1)}, s32[]{:S(2)}) async-start(s8[10485760]{0:T(1024)(128)(4,1)} %bitcast.17), calls=%async_computation | async-start | bytes 4194304
  10.2 14.7 %slice-start.1 = ((s8[10485760]{0:T(1024)(128)(4,1)}), s8[4194304]{0:T(1024)(128)(4,1)S(1)}, s32[]{:S(2)}) async-start(s8[10485760]{0:T(1024)(128)(4,1)} %bitcast.17), calls=%async_computation.1 | async-start | bytes 8388608
  11.7 9.3 %collective-permute-start.7 = (bf16[85,512]{1,0:T(8,128)(2,1)S(1)}, bf16[85,512]{1,0:T(8,128)(2,1)S(1)}, u32[]{:S(2)}, u32[]{:S(2)}) collective-permute-start(bf16[85,512]{1,0:T(8,128)(2,1)S(1)} %fusion.19), channel_id=1, source_target_pairs={{24,0},{28,4},{0,8},{4,12},{8,16},{12,20},{16,24},{20,28},{25,1},{... | collective-permute-start | bytes 261128 | tf_op jit(solution)/shard_map/ppermute | solution.py:15
  14.5 10.4 %slice-start.2 = ((s8[10485760]{0:T(1024)(128)(4,1)}), s8[4194304]{0:T(1024)(128)(4,1)S(1)}, s32[]{:S(2)}) async-start(s8[10485760]{0:T(1024)(128)(4,1)} %bitcast.17), calls=%async_computation.2 | async-start | bytes 8388608
  14.6 6.6 %collective-permute-start.5 = (bf16[85,512]{1,0:T(8,128)(2,1)S(1)}, bf16[85,512]{1,0:T(8,128)(2,1)S(1)}, u32[]{:S(2)}, u32[]{:S(2)}) collective-permute-start(bf16[85,512]{1,0:T(8,128)(2,1)S(1)} %fusion.18), channel_id=1, source_target_pairs={{28,0},{0,4},{4,8},{8,12},{12,16},{16,20},{20,24},{24,28},{29,1},{... | collective-permute-start | bytes 261128 | tf_op jit(solution)/shard_map/ppermute | solution.py:15
  16.3 4.9 %collective-permute-start.3 = (bf16[85,512]{1,0:T(8,128)(2,1)S(1)}, bf16[85,512]{1,0:T(8,128)(2,1)S(1)}, u32[]{:S(2)}, u32[]{:S(2)}) collective-permute-start(bf16[85,512]{1,0:T(8,128)(2,1)S(1)} %fusion.16), channel_id=1, source_target_pairs={{4,0},{8,4},{12,8},{16,12},{20,16},{24,20},{28,24},{0,28},{5,1},{9... | collective-permute-start | bytes 261128 | tf_op jit(solution)/shard_map/ppermute | solution.py:15
  20.3 4.6 %collective-permute-start.1 = (bf16[85,512]{1,0:T(8,128)(2,1)S(1)}, bf16[85,512]{1,0:T(8,128)(2,1)S(1)}, u32[]{:S(2)}, u32[]{:S(2)}) collective-permute-start(bf16[85,512]{1,0:T(8,128)(2,1)S(1)} %fusion.15), channel_id=1, source_target_pairs={{8,0},{12,4},{16,8},{20,12},{24,16},{28,20},{0,24},{4,28},{9,1},{1... | collective-permute-start | bytes 261128 | tf_op jit(solution)/shard_map/ppermute | solution.py:15
  25.0 7.2 %copy-start = (s32[127,512]{1,0:T(8,128)S(1)}, s32[127,512]{1,0:T(8,128)}, u32[]{:S(2)}) copy-start(s32[127,512]{1,0:T(8,128)} %param.10) | copy-start | bytes 780292
  27.5 6.2 %collective-permute-start.10 = (bf16[85,512]{1,0:T(8,128)(2,1)S(1)}, bf16[85,512]{1,0:T(8,128)(2,1)S(1)}, u32[]{:S(2)}, u32[]{:S(2)}) collective-permute-start(bf16[85,512]{1,0:T(8,128)(2,1)S(1)} %get-tuple-element.12), channel_id=1, source_target_pairs={{1,0},{2,1},{3,2},{0,3},{5,4},{6,5},{7,6},{4,7},{9,8},{10,9},{11,1... | collective-permute-start | bytes 261128 | tf_op jit(solution)/shard_map/ppermute | solution.py:15
  31.1 6.4 %collective-permute-start.8 = (bf16[85,512]{1,0:T(8,128)(2,1)S(1)}, bf16[85,512]{1,0:T(8,128)(2,1)S(1)}, u32[]{:S(2)}, u32[]{:S(2)}) collective-permute-start(bf16[85,512]{1,0:T(8,128)(2,1)S(1)} %get-tuple-element.14), channel_id=1, source_target_pairs={{3,0},{0,1},{1,2},{2,3},{7,4},{4,5},{5,6},{6,7},{11,8},{8,9},{9,10... | collective-permute-start | bytes 261128 | tf_op jit(solution)/shard_map/ppermute | solution.py:15
  31.1 7.6 %collective-permute-start.9 = (bf16[85,512]{1,0:T(8,128)(2,1)S(1)}, bf16[85,512]{1,0:T(8,128)(2,1)S(1)}, u32[]{:S(2)}, u32[]{:S(2)}) collective-permute-start(bf16[85,512]{1,0:T(8,128)(2,1)S(1)} %get-tuple-element.13), channel_id=1, source_target_pairs={{2,0},{3,1},{0,2},{1,3},{6,4},{7,5},{4,6},{5,7},{10,8},{11,9},{8,1... | collective-permute-start | bytes 261128 | tf_op jit(solution)/shard_map/ppermute | solution.py:15
  33.7 5.0 %copy-start.1 = (bf16[85,512]{1,0:T(8,128)(2,1)}, bf16[85,512]{1,0:T(8,128)(2,1)S(1)}, u32[]{:S(2)}) copy-start(bf16[85,512]{1,0:T(8,128)(2,1)S(1)} %collective-permute-done.10.refs_3_) | copy-start | bytes 261124
  37.6 1.1 %copy-start.2 = (bf16[85,512]{1,0:T(8,128)(2,1)}, bf16[85,512]{1,0:T(8,128)(2,1)S(1)}, u32[]{:S(2)}) copy-start(bf16[85,512]{1,0:T(8,128)(2,1)S(1)} %collective-permute-done.8.refs_1_) | copy-start | bytes 261124
  38.7 0.6 %copy-start.3 = (bf16[85,512]{1,0:T(8,128)(2,1)}, bf16[85,512]{1,0:T(8,128)(2,1)S(1)}, u32[]{:S(2)}) copy-start(bf16[85,512]{1,0:T(8,128)(2,1)S(1)} %collective-permute-done.9.refs_2_) | copy-start | bytes 261124

commit v3 on v2

--- a/solution.py
+++ b/solution.py
@@ -114,33 +114,36 @@
     depth = (block_count - 1) // 2
     own_group = lax.axis_index("horiz")
     position = (intersection - own_group + depth) % groups
-    collected = []
-    for offset in range(-depth, depth + 1):
-        wanted_group = (own_group + offset) % groups
-        matched = intersection == wanted_group
-        request = jnp.sum(jnp.where(matched[:, None], index_map, 0), axis=0)
-        if offset == 0:
-            collected.append(select_cells(stacked, request))
-        else:
-            incoming = shifted(request, "horiz", offset)
-            outgoing = select_cells(stacked, incoming)
-            collected.append(shifted(outgoing, "horiz", -offset))
+    offsets = range(-depth, depth + 1)
+    requests = {}
+    for offset in offsets:
+        matched = intersection == (own_group + offset) % groups
+        requests[offset] = jnp.sum(jnp.where(matched[:, None], index_map, 0), axis=0)
+    away = [offset for offset in offsets if offset != 0]
+    arrived = {offset: shifted(requests[offset], "horiz", offset) for offset in away}
+    parts = {}
+    for offset in away:
+        outgoing = select_cells(stacked, arrived[offset])
+        parts[offset] = shifted(outgoing, "horiz", -offset)
+    held, requests[0] = lax.optimization_barrier((parts[away[-2]], requests[0]))
+    parts[away[-2]] = held
+    parts[0] = select_cells(stacked, requests[0])
+    collected = [parts[offset] for offset in offsets]
     reach = jnp.repeat(position, index_map.shape[1])[None, :]
     chosen = jnp.zeros((stacked.shape[0], reach.shape[1]), jnp.bfloat16)
     for place, piece in enumerate(collected):
         chosen = jnp.where(reach == place, jnp.concatenate([piece] * block_count, axis=1), chosen)
     weights_flat = blocks.reshape(-1, blocks.shape[2])
-    horizontal = jnp.dot(chosen, weights_flat, preferred_element_type=jnp.float32).astype(
-        jnp.bfloat16
-    )
+    chosen, bracket = lax.optimization_barrier((chosen, bracket))
     shares = lax.axis_size("lev")
     own_share = lax.axis_index("lev")
     width = blocks.shape[2] // shares
-    slabs = []
-    for distance in range(shares):
+    slabs = [None] * shares
+    for distance in [shares // 2] + [d for d in range(1, shares) if d != shares // 2] + [0]:
         target = (own_share + distance) % shares
-        part = lax.dynamic_slice_in_dim(horizontal, target * width, width, axis=1)
-        slabs.append(part if distance == 0 else shifted(part, "lev", distance))
+        columns = lax.dynamic_slice_in_dim(weights_flat, target * width, width, axis=1)
+        part = jnp.dot(chosen, columns, preferred_element_type=jnp.float32).astype(jnp.bfloat16)
+        slabs[distance] = part if distance == 0 else shifted(part, "lev", distance)
 
     def place(level):
         return (own_share - level // level_slab) % shares * level_slab + level % level_slab

time: 43.8 us -> 41.4 us (0.945)
  waiting for transfers between devices: 8.54 us -> 5.15 us
  matrix products: 9.28 us -> 10.3 us
  local copies, waits for them, and re-layouts: 3.44 us -> 2.8 us
    ppermute x11, waiting for transfers between devices: 8.54 us -> 5.15 us  [shifted(): return lax.ppermute(block, axis, route)]
    dot_general x1 -> x4, matrix products: 1.88 us -> 2.94 us  [local(): jnp.dot(chosen, columns, preferred_element_type=jnp.float32)]
    dynamic_slice x1 -> x0, local copies, waits for them, and re-layouts: 0.66 us -> none  [local(): part = lax.dynamic_slice_in_dim(horizontal, target * width, width, axis=1)]
  transfers between devices with their start and end apart: 11 -> 11, of which waited for: 3 -> 2; matrix products, arithmetic and copies ran while one was open for 25% -> 30% of each run, Pallas kernels for 0% -> 0%
where the time goes in v3:
time: 41.4 us; the launch traced here: 41.1 us
  starting transfers between devices  14.9 us (36%)
  matrix products  10.3 us (25%)
  waiting for transfers between devices  5.15 us (12%)
  Pallas kernels  4.28 us (10%)
  other arithmetic  3.32 us (8%)
  local copies, waits for them, and re-layouts  2.8 us (7%)
    ppermute x11, starting transfers between devices, shifted(): return lax.ppermute(block, axis, route)  14.9 us
    dot_general x5, matrix products, select_cells(): jnp.dot(tile, picker, preferred_element_type=jnp.float32)  7.4 us
    ppermute x11, waiting for transfers between devices, shifted(): return lax.ppermute(block, axis, route)  5.15 us
    pallas_call x1, Pallas kernels, interpolate(): pl.pallas_call(interpolate_body, out_shape=jax.ShapeDtypeStruct((fields,...  4.28 us
    dot_general x4, matrix products, local(): jnp.dot(chosen, columns, preferred_element_type=jnp.float32)  2.94 us
    add x1, other arithmetic, place(): (own_share - level // level_slab) % shares * level_slab + level % level_slab  1.54 us
    reshape x1, local copies, waits for them, and re-layouts, local(): stacked = source_state.reshape(fields * level_slab, tile_cells)  1.45 us
    unnamed x33, local copies, waits for them, and re-layouts  0.84 us
  transfers between devices with their start and end apart: 11, of which 2 were waited for; matrix products, arithmetic and copies ran while one was open for 30% of the time, Pallas kernels for 0%

profile of v3, /device:TPU:0, one launch (start us, length us, event | category | flops | bytes accessed | tf_op | source)
XLA Modules:
  0.0 41.1 jit_solution(11078356746356353789)
XLA Ops:
  0.0 0.7 %broadcast_compare_fusion.7 = (pred[5]{0:T(512)(128)(4,1)S(1)}, s32[5]{0:T(128)S(1)}, pred[5]{0:T(512)(128)(4,1)S(1)}, pred[5]{0:T(512)(128)(4,1)S(1)}, pred[5]{...) fusion(s32[5]{0:T(128)} %param.7, s32[]{:T(128)S(6)} %axis_index.25, s32[]{:T(128)S(6)} %select_n.120, ...), kind=kLoop, calls=%fused_computation.105 | loop fusion | flops 95 | bytes 94 | tf_op jit(solution)/shard_map/eq | solution.py:135
  0.7 0.8 %select_reduce_fusion = (s32[512]{0:T(512)S(1)}, s32[512]{0:T(512)S(1)}, s32[512]{0:T(512)S(1)}, s32[512]{0:T(512)S(1)}, s32[512]{0:T(512)S(1)}) fusion(s32[5,512]{1,0:T(8,128)} %param.8, pred[5]{0:T(512)(128)(4,1)S(1)} %get-tuple-element.29, pred[5]{0:T(512)(128)(4,1)S(1)} %get-tuple-element.26, pred[5]{0:T(512)(128)(4,1)S(1)} %get-tuple-element.27, ...), kind=kLoop, calls=%fused_computation.85 | loop fusion | flops 23040 | bytes 20505 | tf_op jit(solution)/shard_map/reduce_sum | solution.py:121
  1.5 4.0 %collective-permute-start.6 = (s32[512]{0:T(512)S(1)}, s32[512]{0:T(512)S(1)}, u32[]{:S(2)}, u32[]{:S(2)}) collective-permute-start(s32[512]{0:T(512)S(1)} %get-tuple-element.13), channel_id=1, source_target_pairs={{8,0},{12,4},{16,8},{20,12},{24,16},{28,20},{0,24},{4,28},{9,1},{1... | collective-permute-start | bytes 6152 | tf_op jit(solution)/shard_map/ppermute | solution.py:15
  5.5 2.6 %collective-permute-start.4 = (s32[512]{0:T(512)S(1)}, s32[512]{0:T(512)S(1)}, u32[]{:S(2)}, u32[]{:S(2)}) collective-permute-start(s32[512]{0:T(512)S(1)} %get-tuple-element.17), channel_id=1, source_target_pairs={{4,0},{8,4},{12,8},{16,12},{20,16},{24,20},{28,24},{0,28},{5,1},{9... | collective-permute-start | bytes 6152 | tf_op jit(solution)/shard_map/ppermute | solution.py:15
  8.1 0.1 broadcast_in_dim.97
  8.2 0.1 broadcast_in_dim.93
  8.3 0.1 broadcast_in_dim.103
  8.4 0.1 broadcast_in_dim.101
  8.5 0.1 broadcast_in_dim.106
  8.6 1.4 %reshape.61 = bf16[85,4096]{1,0:T(8,128)(2,1)S(1)} reshape(bf16[5,17,4096]{2,1,0:T(8,128)(2,1)} %param.6) | data formatting | bytes 1392640 | tf_op jit(solution)/shard_map/reshape | solution.py:111
  10.1 1.5 %fusion.35 = bf16[85,512]{1,0:T(8,128)(2,1)S(1)} fusion(bf16[85,4096]{1,0:T(8,128)(2,1)S(1)} %reshape.61, s32[512]{0:T(512)S(1)} %collective-permute-done), kind=kOutput, calls=%fused_computation.32 | convolution fusion | flops 358656512 | bytes 785408 | tf_op jit(solution)/shard_map/dot_general | solution.py:21
  11.6 1.8 %collective-permute-start.1 = (bf16[85,512]{1,0:T(8,128)(2,1)S(1)}, bf16[85,512]{1,0:T(8,128)(2,1)S(1)}, u32[]{:S(2)}, u32[]{:S(2)}) collective-permute-start(bf16[85,512]{1,0:T(8,128)(2,1)S(1)} %fusion.35), channel_id=1, source_target_pairs={{8,0},{12,4},{16,8},{20,12},{24,16},{28,20},{0,24},{4,28},{9,1},{1... | collective-permute-start | bytes 261128 | tf_op jit(solution)/shard_map/ppermute | solution.py:15
  13.4 1.5 %fusion.36 = bf16[85,512]{1,0:T(8,128)(2,1)S(1)} fusion(bf16[85,4096]{1,0:T(8,128)(2,1)S(1)} %reshape.61, s32[512]{0:T(512)S(1)} %collective-permute-done.2), kind=kOutput, calls=%fused_computation.33 | convolution fusion | flops 358656512 | bytes 785408 | tf_op jit(solution)/shard_map/dot_general | solution.py:21
  14.9 0.1 collective-permute-start.3
  14.9 1.5 %fusion.38 = bf16[85,512]{1,0:T(8,128)(2,1)S(1)} fusion(bf16[85,4096]{1,0:T(8,128)(2,1)S(1)} %reshape.61, s32[512]{0:T(512)S(1)} %collective-permute-done.4), kind=kOutput, calls=%fused_computation.35 | convolution fusion | flops 358656512 | bytes 785408 | tf_op jit(solution)/shard_map/dot_general | solution.py:21
  16.4 0.5 %collective-permute-start.5 = (bf16[85,512]{1,0:T(8,128)(2,1)S(1)}, bf16[85,512]{1,0:T(8,128)(2,1)S(1)}, u32[]{:S(2)}, u32[]{:S(2)}) collective-permute-start(bf16[85,512]{1,0:T(8,128)(2,1)S(1)} %fusion.38), channel_id=1, source_target_pairs={{28,0},{0,4},{4,8},{8,12},{12,16},{16,20},{20,24},{24,28},{29,1},{... | collective-permute-start | bytes 261128 | tf_op jit(solution)/shard_map/ppermute | solution.py:15
  17.0 1.5 %fusion.39 = bf16[85,512]{1,0:T(8,128)(2,1)S(1)} fusion(bf16[85,4096]{1,0:T(8,128)(2,1)S(1)} %reshape.61, s32[512]{0:T(512)S(1)} %collective-permute-done.6), kind=kOutput, calls=%fused_computation.36 | convolution fusion | flops 358656512 | bytes 785408 | tf_op jit(solution)/shard_map/dot_general | solution.py:21
  18.5 0.3 collective-permute-start.7
  18.8 1.5 %constant_dynamic-update-slice_fusion.14 = (bf16[85,2560]{1,0:T(8,128)(2,1)S(1)}, bf16[85,512]{1,0:T(8,128)(2,1)S(1)}) fusion(bf16[85,4096]{1,0:T(8,128)(2,1)S(1)} %reshape.61, s32[512]{0:T(512)S(1)} %get-tuple-element.10), kind=kOutput, calls=%fused_computation.74 | convolution fusion | flops 358656512 | bytes 878592 | tf_op jit(solution)/shard_map/dot_general | solution.py:21
  20.4 3.6 %collective-permute-done.7 = bf16[85,512]{1,0:T(8,128)(2,1)S(1)} collective-permute-done((bf16[85,512]{1,0:T(8,128)(2,1)S(1)}, bf16[85,512]{1,0:T(8,128)(2,1)S(1)}, u32[]{:S(2)}, u32[]{:S(2)}) %collective-permute-start.7) | collective-permute-done | bytes 87072 | tf_op jit(solution)/shard_map/ppermute | solution.py:15
  24.2 0.3 select_select_fusion
  24.6 0.6 %fusion.27 = bf16[85,512]{1,0:T(8,128)(2,1)S(1)} fusion(bf16[85,2560]{1,0:T(8,128)(2,1)S(1)} %select_select_fusion, bf16[2560,2048]{1,0:T(8,128)(2,1)S(1)} %bitcast.22, s32[]{:T(128)S(6)} %select_n.144), kind=kOutput, calls=%fused_computation.26 | convolution fusion | flops 222865920 | bytes 3159044 | tf_op jit(solution)/shard_map/dot_general | solution.py:145
  25.1 0.6 %fusion.24 = bf16[85,512]{1,0:T(8,128)(2,1)S(1)} fusion(bf16[85,2560]{1,0:T(8,128)(2,1)S(1)} %select_select_fusion, bf16[2560,2048]{1,0:T(8,128)(2,1)S(1)} %bitcast.23, s32[]{:T(128)S(6)} %select_n.142), kind=kOutput, calls=%fused_computation.25 | convolution fusion | flops 222865920 | bytes 3159044 | tf_op jit(solution)/shard_map/dot_general | solution.py:145
  25.7 0.6 %fusion.21 = bf16[85,512]{1,0:T(8,128)(2,1)S(1)} fusion(bf16[85,2560]{1,0:T(8,128)(2,1)S(1)} %select_select_fusion, bf16[2560,2048]{1,0:T(8,128)(2,1)S(1)} %bitcast.24, s32[]{:T(128)S(6)} %select_n.140), kind=kOutput, calls=%fused_computation.24 | convolution fusion | flops 222865920 | bytes 3159044 | tf_op jit(solution)/shard_map/dot_general | solution.py:145
  26.3 1.6 %collective-permute-start.8 = (bf16[85,512]{1,0:T(8,128)(2,1)S(1)}, bf16[85,512]{1,0:T(8,128)(2,1)S(1)}, u32[]{:S(2)}, u32[]{:S(2)}) collective-permute-start(bf16[85,512]{1,0:T(8,128)(2,1)S(1)} %fusion.21), channel_id=1, source_target_pairs={{3,0},{0,1},{1,2},{2,3},{7,4},{4,5},{5,6},{6,7},{11,8},{8,9},{9,10... | collective-permute-start | bytes 261128 | tf_op jit(solution)/shard_map/ppermute | solution.py:15
  27.9 2.6 %collective-permute-start.9 = (bf16[85,512]{1,0:T(8,128)(2,1)S(1)}, bf16[85,512]{1,0:T(8,128)(2,1)S(1)}, u32[]{:S(2)}, u32[]{:S(2)}) collective-permute-start(bf16[85,512]{1,0:T(8,128)(2,1)S(1)} %fusion.24), channel_id=1, source_target_pairs={{2,0},{3,1},{0,2},{1,3},{6,4},{7,5},{4,6},{5,7},{10,8},{11,9},{8,1... | collective-permute-start | bytes 261128 | tf_op jit(solution)/shard_map/ppermute | solution.py:15
  30.5 1.4 %collective-permute-start.10 = (bf16[85,512]{1,0:T(8,128)(2,1)S(1)}, bf16[85,512]{1,0:T(8,128)(2,1)S(1)}, u32[]{:S(2)}, u32[]{:S(2)}) collective-permute-start(bf16[85,512]{1,0:T(8,128)(2,1)S(1)} %fusion.27), channel_id=1, source_target_pairs={{1,0},{2,1},{3,2},{0,3},{5,4},{6,5},{7,6},{4,7},{9,8},{10,9},{11,1... | collective-permute-start | bytes 261128 | tf_op jit(solution)/shard_map/ppermute | solution.py:15
  31.9 1.5 %fusion.47 = (s32[127,512]{1,0:T(8,128)}, s32[127,512]{1,0:T(8,128)}) fusion(s32[127,512]{1,0:T(8,128)S(1)} %copy-done, s32[]{:T(128)S(6)} %axis_index.22), kind=kLoop, calls=%fused_computation.55 | loop fusion | flops 3446272 | bytes 780292 | tf_op jit(solution)/shard_map/add | solution.py:149
  33.4 1.2 %fusion.18.refs_0_ = bf16[85,512]{1,0:T(8,128)(2,1)} fusion(bf16[85,2560]{1,0:T(8,128)(2,1)S(1)} %select_select_fusion, bf16[2560,2048]{1,0:T(8,128)(2,1)S(1)} %bitcast.25, s32[]{:T(128)S(6)} %select_n.138), kind=kOutput, calls=%fused_computation.23 | convolution fusion | flops 222865920 | bytes 3159044 | tf_op jit(solution)/shard_map/dot_general | solution.py:145
  34.6 1.6 %collective-permute-done.9.refs_2_ = bf16[85,512]{1,0:T(8,128)(2,1)S(1)} collective-permute-done((bf16[85,512]{1,0:T(8,128)(2,1)S(1)}, bf16[85,512]{1,0:T(8,128)(2,1)S(1)}, u32[]{:S(2)}, u32[]{:S(2)}) %collective-permute-start.9) | collective-permute-done | bytes 87072 | tf_op jit(solution)/shard_map/ppermute | solution.py:15
  36.2 0.6 %copy-done.2 = bf16[85,512]{1,0:T(8,128)(2,1)} copy-done((bf16[85,512]{1,0:T(8,128)(2,1)}, bf16[85,512]{1,0:T(8,128)(2,1)S(1)}, u32[]{:S(2)}) %copy-start.2) | copy-done | bytes 87064
  36.9 4.3 %interpolate.1 = bf16[5,127,512]{2,1,0:T(8,128)(2,1)} custom-call(s32[127,512]{1,0:T(8,128)} %get-tuple-element.21.lower_ref, s32[127,512]{1,0:T(8,128)} %get-tuple-element.20.upper_ref, f32[127,512]{1,0:T(8,128)} %fraction_ref.1, bf16[85,512]{1,0:T(8,128)(2,1)} %fusion.18.refs_0_, bf16[85,512]{1,0:T(8,128)(2,1)} %copy-done.1, bf16[85,512]{1,0:T(8,128)(2,1)} %copy-done.2, ...), custom_call_target="tpu_custom_call" | custom-call | tf_op jit(solution)/shard_map/interpolate/pallas_call | solution.py:99
  (54 shorter events, 0.4 us)
Async XLA Ops:
  1.5 15.5 %collective-permute-start.6 = (s32[512]{0:T(512)S(1)}, s32[512]{0:T(512)S(1)}, u32[]{:S(2)}, u32[]{:S(2)}) collective-permute-start(s32[512]{0:T(512)S(1)} %get-tuple-element.13), channel_id=1, source_target_pairs={{8,0},{12,4},{16,8},{20,12},{24,16},{28,20},{0,24},{4,28},{9,1},{1... | collective-permute-start | bytes 6152 | tf_op jit(solution)/shard_map/ppermute | solution.py:15
  5.5 7.9 %collective-permute-start.2 = (s32[512]{0:T(512)S(1)}, s32[512]{0:T(512)S(1)}, u32[]{:S(2)}, u32[]{:S(2)}) collective-permute-start(s32[512]{0:T(512)S(1)} %get-tuple-element.15), channel_id=1, source_target_pairs={{28,0},{0,4},{4,8},{8,12},{12,16},{16,20},{20,24},{24,28},{29,1},{... | collective-permute-start | bytes 6152 | tf_op jit(solution)/shard_map/ppermute | solution.py:15
  5.5 4.6 %collective-permute-start = (s32[512]{0:T(512)S(1)}, s32[512]{0:T(512)S(1)}, u32[]{:S(2)}, u32[]{:S(2)}) collective-permute-start(s32[512]{0:T(512)S(1)} %get-tuple-element.16), channel_id=1, source_target_pairs={{24,0},{28,4},{0,8},{4,12},{8,16},{12,20},{16,24},{20,28},{25,1},{... | collective-permute-start | bytes 6152 | tf_op jit(solution)/shard_map/ppermute | solution.py:15
  5.5 9.5 %collective-permute-start.4 = (s32[512]{0:T(512)S(1)}, s32[512]{0:T(512)S(1)}, u32[]{:S(2)}, u32[]{:S(2)}) collective-permute-start(s32[512]{0:T(512)S(1)} %get-tuple-element.17), channel_id=1, source_target_pairs={{4,0},{8,4},{12,8},{16,12},{20,16},{24,20},{28,24},{0,28},{5,1},{9... | collective-permute-start | bytes 6152 | tf_op jit(solution)/shard_map/ppermute | solution.py:15
  11.6 12.6 %collective-permute-start.1 = (bf16[85,512]{1,0:T(8,128)(2,1)S(1)}, bf16[85,512]{1,0:T(8,128)(2,1)S(1)}, u32[]{:S(2)}, u32[]{:S(2)}) collective-permute-start(bf16[85,512]{1,0:T(8,128)(2,1)S(1)} %fusion.35), channel_id=1, source_target_pairs={{8,0},{12,4},{16,8},{20,12},{24,16},{28,20},{0,24},{4,28},{9,1},{1... | collective-permute-start | bytes 261128 | tf_op jit(solution)/shard_map/ppermute | solution.py:15
  13.4 11.1 %slice-start = ((s8[10485760]{0:T(1024)(128)(4,1)}), s8[4194304]{0:T(1024)(128)(4,1)S(1)}, s32[]{:S(2)}) async-start(s8[10485760]{0:T(1024)(128)(4,1)} %bitcast.20), calls=%async_computation | async-start | bytes 8388608
  14.9 9.7 %slice-start.1 = ((s8[10485760]{0:T(1024)(128)(4,1)}), s8[4194304]{0:T(1024)(128)(4,1)S(1)}, s32[]{:S(2)}) async-start(s8[10485760]{0:T(1024)(128)(4,1)} %bitcast.20), calls=%async_computation.1 | async-start | bytes 8388608
  14.9 3.9 %collective-permute-start.3 = (bf16[85,512]{1,0:T(8,128)(2,1)S(1)}, bf16[85,512]{1,0:T(8,128)(2,1)S(1)}, u32[]{:S(2)}, u32[]{:S(2)}) collective-permute-start(bf16[85,512]{1,0:T(8,128)(2,1)S(1)} %fusion.36), channel_id=1, source_target_pairs={{4,0},{8,4},{12,8},{16,12},{20,16},{24,20},{28,24},{0,28},{5,1},{9... | collective-permute-start | bytes 261128 | tf_op jit(solution)/shard_map/ppermute | solution.py:15
  16.4 7.6 %collective-permute-start.5 = (bf16[85,512]{1,0:T(8,128)(2,1)S(1)}, bf16[85,512]{1,0:T(8,128)(2,1)S(1)}, u32[]{:S(2)}, u32[]{:S(2)}) collective-permute-start(bf16[85,512]{1,0:T(8,128)(2,1)S(1)} %fusion.38), channel_id=1, source_target_pairs={{28,0},{0,4},{4,8},{8,12},{12,16},{16,20},{20,24},{24,28},{29,1},{... | collective-permute-start | bytes 261128 | tf_op jit(solution)/shard_map/ppermute | solution.py:15
  18.5 5.5 %collective-permute-start.7 = (bf16[85,512]{1,0:T(8,128)(2,1)S(1)}, bf16[85,512]{1,0:T(8,128)(2,1)S(1)}, u32[]{:S(2)}, u32[]{:S(2)}) collective-permute-start(bf16[85,512]{1,0:T(8,128)(2,1)S(1)} %fusion.39), channel_id=1, source_target_pairs={{24,0},{28,4},{0,8},{4,12},{8,16},{12,20},{16,24},{20,28},{25,1},{... | collective-permute-start | bytes 261128 | tf_op jit(solution)/shard_map/ppermute | solution.py:15
  18.8 5.8 %slice-start.2 = ((s8[10485760]{0:T(1024)(128)(4,1)}), s8[2097152]{0:T(1024)(128)(4,1)S(1)}, s32[]{:S(2)}) async-start(s8[10485760]{0:T(1024)(128)(4,1)} %bitcast.20), calls=%async_computation.2 | async-start | bytes 4194304
  20.3 11.6 %copy-start = (s32[127,512]{1,0:T(8,128)S(1)}, s32[127,512]{1,0:T(8,128)}, u32[]{:S(2)}) copy-start(s32[127,512]{1,0:T(8,128)} %param.10) | copy-start | bytes 780292
  26.3 8.3 %collective-permute-start.8 = (bf16[85,512]{1,0:T(8,128)(2,1)S(1)}, bf16[85,512]{1,0:T(8,128)(2,1)S(1)}, u32[]{:S(2)}, u32[]{:S(2)}) collective-permute-start(bf16[85,512]{1,0:T(8,128)(2,1)S(1)} %fusion.21), channel_id=1, source_target_pairs={{3,0},{0,1},{1,2},{2,3},{7,4},{4,5},{5,6},{6,7},{11,8},{8,9},{9,10... | collective-permute-start | bytes 261128 | tf_op jit(solution)/shard_map/ppermute | solution.py:15
  27.9 8.3 %collective-permute-start.9 = (bf16[85,512]{1,0:T(8,128)(2,1)S(1)}, bf16[85,512]{1,0:T(8,128)(2,1)S(1)}, u32[]{:S(2)}, u32[]{:S(2)}) collective-permute-start(bf16[85,512]{1,0:T(8,128)(2,1)S(1)} %fusion.24), channel_id=1, source_target_pairs={{2,0},{3,1},{0,2},{1,3},{6,4},{7,5},{4,6},{5,7},{10,8},{11,9},{8,1... | collective-permute-start | bytes 261128 | tf_op jit(solution)/shard_map/ppermute | solution.py:15
  30.5 5.7 %collective-permute-start.10 = (bf16[85,512]{1,0:T(8,128)(2,1)S(1)}, bf16[85,512]{1,0:T(8,128)(2,1)S(1)}, u32[]{:S(2)}, u32[]{:S(2)}) collective-permute-start(bf16[85,512]{1,0:T(8,128)(2,1)S(1)} %fusion.27), channel_id=1, source_target_pairs={{1,0},{2,1},{3,2},{0,3},{5,4},{6,5},{7,6},{4,7},{9,8},{10,9},{11,1... | collective-permute-start | bytes 261128 | tf_op jit(solution)/shard_map/ppermute | solution.py:15
  34.6 1.6 %copy-start.1 = (bf16[85,512]{1,0:T(8,128)(2,1)}, bf16[85,512]{1,0:T(8,128)(2,1)S(1)}, u32[]{:S(2)}) copy-start(bf16[85,512]{1,0:T(8,128)(2,1)S(1)} %collective-permute-done.8.refs_1_) | copy-start | bytes 261124
  36.2 0.6 %copy-start.2 = (bf16[85,512]{1,0:T(8,128)(2,1)}, bf16[85,512]{1,0:T(8,128)(2,1)S(1)}, u32[]{:S(2)}) copy-start(bf16[85,512]{1,0:T(8,128)(2,1)S(1)} %collective-permute-done.9.refs_2_) | copy-start | bytes 261124
  36.2 0.7 %copy-start.3 = (bf16[85,512]{1,0:T(8,128)(2,1)}, bf16[85,512]{1,0:T(8,128)(2,1)S(1)}, u32[]{:S(2)}) copy-start(bf16[85,512]{1,0:T(8,128)(2,1)S(1)} %collective-permute-done.10.refs_3_) | copy-start | bytes 261124
